TPU v7x, 512 devices: a 8x2x16 block of a 8x8x16 slice. The times are simulated.
512 devices in a mesh: groups: 2 (over y), context: 128 (over z, x), tensor: 2 (over core).
Axes of the slice: x: 8, y: 2, z: 16, core: 2. Of those that a mesh axis runs over, the one named last changes fastest.
The devices are a block of a 8x8x16 slice.
Arguments:
- self_queries: bfloat16 [20480, 2048], P(('groups', 'context'), 'tensor'), parts along dimension 0, may hold values from -512 to 512
- self_keys: bfloat16 [20480, 512], P(('groups', 'context'), 'tensor'), parts along dimension 0, may hold values from -6 to 6
- self_values: bfloat16 [20480, 512], P(('groups', 'context'), 'tensor'), parts along dimension 0, may hold values from -6 to 6
- cross_queries: bfloat16 [20480, 2048], P(('groups', 'context'), 'tensor'), parts along dimension 0, may hold values from -512 to 512
- cross_keys: bfloat16 [6144, 512], P(('groups', 'context'), 'tensor'), parts along dimension 0, may hold values from -6 to 6
- cross_values: bfloat16 [6144, 512], P(('groups', 'context'), 'tensor'), parts along dimension 0, may hold values from -6 to 6
- span_order: int32 [512], P('groups'), parts along dimension 0, may hold values from 0 to 255, as said below
Outputs:
- self_out: bfloat16 [20480, 2048], P(('groups', 'context'), 'tensor'), parts along dimension 0
- cross_out: bfloat16 [20480, 2048], P(('groups', 'context'), 'tensor'), parts along dimension 0
There are 2 independent parts, one for each index of `groups`. A program takes and returns all parts, laid end to end along the dimension named above; each array names one. Nothing has to cross between parts.
Inputs may be any that keep to these rules, and one draw needn't show every extreme that they name: `span_order`: each of 0 to 255 appears once, and entries 2 d and 2 d + 1 sum to 255.
All inputs are finite; a program needn't handle non-finite values.
Results may differ from a plain program's by a relative error of at most 0.012.
The roundings to bfloat16 on the way count: a program that leaves them out, or rounds other values in their place, can miss the bound.
Values may be sent and summed in bfloat16 or wider, within the bound.
No kernel may reach another device: no remote copies, remote signals or barrier semaphores. Data moves between devices by JAX's collectives and lax.ppermute only.
A program may use at most 128 MiB of HBM per device.

v0:
```python
import jax
import jax.numpy as jnp
from jax import lax
from jax.sharding import PartitionSpec as P

HEAD_DIM = 128
HEADS = 16
KV_HEADS = 4


NEG_FILL = -1e30


def in_order(pieces, dim):
    shape = list(pieces.shape[1:])
    shape[dim] *= pieces.shape[0]
    return jnp.moveaxis(pieces, 0, dim).reshape(shape)


def one_gather(arrays, axis, dims):
    line = jnp.concatenate([a.reshape(-1) for a in arrays])
    lines, at, finished = (lax.all_gather(line, axis), 0, [])
    for a, dim in zip(arrays, dims):
        pieces = lines[:, at : at + a.size].reshape(-1, *a.shape)
        finished.append(in_order(pieces, dim))
        at += a.size
    return tuple(finished)


def rotary(values, places):
    half_dim = values.shape[-1] // 2
    frequency = 500000.0 ** (-(jnp.arange(half_dim, dtype=jnp.float32) * 2.0) / values.shape[-1])
    angles = places.astype(jnp.float32)[:, None] * frequency[None, :]
    cosine = jnp.cos(angles)[:, None, :]
    sine_part = jnp.sin(angles)[:, None, :]
    first_half = values[..., :half_dim]
    second_half = values[..., half_dim:]
    return jnp.concatenate(
        [
            first_half * cosine - second_half * sine_part,
            second_half * cosine + first_half * sine_part,
        ],
        -1,
    )


def update_rows(carry_state, queries, query_places, key_rows, value_rows, key_places):
    row_peak, weight_sum, mixed_sum = carry_state
    scores = jnp.einsum(
        "qkgd,rkd->kgqr", queries, key_rows, preferred_element_type=jnp.float32
    ) * queries.shape[-1] ** (-0.5)
    if key_places is not None:
        allowed = (key_places[None, :] <= query_places[:, None])[None, None]
        scores = jnp.where(allowed, scores, NEG_FILL)
    new_peak = jnp.maximum(row_peak, jnp.max(scores, -1))
    weights = jnp.exp(scores - new_peak[..., None])
    if key_places is not None:
        weights = jnp.where(allowed, weights, 0.0)
    factor = jnp.exp(row_peak - new_peak)
    weight_sum = weight_sum * factor + jnp.sum(weights, -1)
    mixed_sum = mixed_sum * factor[..., None] + jnp.einsum(
        "kgqr,rkd->kgqd",
        weights.astype(jnp.bfloat16),
        value_rows,
        preferred_element_type=jnp.float32,
    )
    return (new_peak, weight_sum, mixed_sum)


def advance(carry_state, queries, query_places, key_rows, value_rows, key_places):
    if key_places is None:
        return update_rows(carry_state, queries, query_places, key_rows, value_rows, None)
    return update_rows(carry_state, queries, query_places, key_rows, value_rows, key_places)


def sweep_keys(carry_state, queries, query_places, key_rows, value_rows, key_places):
    row_total = key_rows.shape[0]
    block_rows = row_total
    while block_rows > 512 and block_rows % 2 == 0:
        block_rows = block_rows // 2
    block_count = row_total // block_rows
    key_blocks = key_rows.reshape((block_count, block_rows) + key_rows.shape[1:])
    value_blocks = value_rows.reshape((block_count, block_rows) + value_rows.shape[1:])
    if key_places is None:

        def plain_step(inner_state, arrived):
            return (advance(inner_state, queries, query_places, arrived[0], arrived[1], None), None)

        final_state, unused = lax.scan(plain_step, carry_state, (key_blocks, value_blocks))
    else:
        place_blocks = key_places.reshape(block_count, block_rows)

        def masked_step(inner_state, arrived):
            return (
                advance(inner_state, queries, query_places, arrived[0], arrived[1], arrived[2]),
                None,
            )

        final_state, unused = lax.scan(
            masked_step, carry_state, (key_blocks, value_blocks, place_blocks)
        )
    return final_state


def finish(carry_state):
    row_peak, weight_sum, mixed_sum = carry_state
    result = mixed_sum / weight_sum[..., None]
    result = jnp.transpose(result, (2, 0, 1, 3))
    return result.reshape(result.shape[0], -1).astype(jnp.bfloat16)


def body(self_queries, self_keys, self_values, cross_queries, cross_keys, cross_values, span_order):
    local_rows = self_queries.shape[0]
    span_len = local_rows // 2
    kv_local = self_keys.shape[1] // HEAD_DIM
    group_size = HEADS // KV_HEADS
    device = lax.axis_index("context")
    owned_spans = lax.dynamic_slice(span_order, (2 * device,), (2,))
    within_span = jnp.arange(span_len, dtype=jnp.int32)[None, :]
    query_places = (owned_spans[:, None] * span_len + within_span).reshape(-1)
    text_queries = rotary(
        self_queries.astype(jnp.float32).reshape(local_rows, kv_local * group_size, HEAD_DIM),
        query_places,
    )
    text_queries = text_queries.astype(jnp.bfloat16).reshape(
        local_rows, kv_local, group_size, HEAD_DIM
    )
    text_keys = rotary(
        self_keys.astype(jnp.float32).reshape(local_rows, kv_local, HEAD_DIM), query_places
    )
    text_keys = text_keys.astype(jnp.bfloat16).reshape(local_rows, kv_local * HEAD_DIM)
    image_queries = cross_queries.reshape(local_rows, kv_local, group_size, HEAD_DIM)
    empty_state = (
        jnp.full((kv_local, group_size, local_rows), NEG_FILL, jnp.float32),
        jnp.zeros((kv_local, group_size, local_rows), jnp.float32),
        jnp.zeros((kv_local, group_size, local_rows, HEAD_DIM), jnp.float32),
    )
    every_text_keys, every_text_values, every_image_keys, every_image_values = one_gather(
        (text_keys, self_values, cross_keys, cross_values), "context", (0, 0, 0, 0)
    )
    span_total = span_order.shape[0]
    inverse_order = (
        jnp.zeros((span_total,), jnp.int32)
        .at[span_order]
        .set(jnp.arange(span_total, dtype=jnp.int32))
    )
    ordered_keys = jnp.take(
        every_text_keys.reshape(span_total, span_len, -1), inverse_order, axis=0
    )
    ordered_values = jnp.take(
        every_text_values.reshape(span_total, span_len, -1), inverse_order, axis=0
    )
    every_places = jnp.arange(span_total * span_len, dtype=jnp.int32)
    self_state = sweep_keys(
        empty_state,
        text_queries,
        query_places,
        ordered_keys.reshape(-1, kv_local, HEAD_DIM),
        ordered_values.reshape(-1, kv_local, HEAD_DIM),
        every_places,
    )
    cross_state = sweep_keys(
        empty_state,
        image_queries,
        None,
        every_image_keys.reshape(-1, kv_local, HEAD_DIM),
        every_image_values.reshape(-1, kv_local, HEAD_DIM),
        None,
    )
    return (finish(self_state), finish(cross_state))


def solution(mesh):
    in_specs = (
        P(("groups", "context"), "tensor"),
        P(("groups", "context"), "tensor"),
        P(("groups", "context"), "tensor"),
        P(("groups", "context"), "tensor"),
        P(("groups", "context"), "tensor"),
        P(("groups", "context"), "tensor"),
        P("groups"),
    )
    out_specs = (P(("groups", "context"), "tensor"), P(("groups", "context"), "tensor"))
    return jax.shard_map(body, mesh=mesh, in_specs=in_specs, out_specs=out_specs, check_vma=False)
```

profile of v0, /device:TPU:65, one launch (start us, length us, event | category | flops | bytes accessed | tf_op | source)
XLA Modules:
  0.0 424.0 jit_solution(2575572624039003059)
XLA Ops:
  15.3 1.6 scatter_custom_fusion
  17.4 198.0 %all-gather.3.cloned.1.call-done = bf16[6815744]{0:T(1024)(128)(2,1)} async-done(((bf16[53248]{0:T(1024)(128)(2,1)}), bf16[6815744]{0:T(1024)(128)(2,1)}) %all-gather.3.cloned.1.call-update) | async-done | bytes 13631504 | tf_op jit(solution)/shard_map/all_gather | solution.py:22
  215.4 17.8 %reshape.198 = bf16[128,53248]{1,0:T(8,128)(2,1)} reshape(bf16[6815744]{0:T(1024)(128)(2,1)} %all-gather.3.cloned.1.call-done) | data formatting | bytes 27262976 | tf_op jit(solution)/shard_map/all_gather | solution.py:22
  233.3 3.4 fusion.24
  236.6 9.0 %fusion.25 = (bf16[128,20480]{1,0:T(8,128)(2,1)}, bf16[128,20480]{1,0:T(8,128)(2,1)}) fusion(bf16[128,53248]{1,0:T(8,128)(2,1)} %reshape.198), kind=kLoop, calls=%fused_computation.72 | loop fusion | bytes 20971520 | tf_op jit(solution)/shard_map/slice | solution.py:24
  245.7 4.9 %reshape_reshape_reshape_reshape.6 = bf16[8,384,2,128]{3,2,1,0:T(2,128)(2,1)} reshape(bf16[128,6144]{1,0:T(8,128)(2,1)} %get-tuple-element.227) | data formatting | bytes 3145728 | tf_op jit(solution)/shard_map/reshape;reshape;reshape;reshape | solution.py:82
  250.6 2.0 reshape_reshape_reshape_reshape.7
  252.6 20.3 %while.31 = (s32[]{:T(128)}, f32[2,4,80]{2,1,0:T(4,128)S(1)}, f32[2,4,80]{2,1,0:T(4,128)S(1)}, f32[2,4,80,128]{3,2,1,0:T(8,128)S(1)}, bf16[8,384,2,128]{3,2,1,0:...) while((s32[]{:T(128)}, f32[2,4,80]{2,1,0:T(4,128)S(1)}, ...), condition=%wide.region_8.10_spmd.clone, body=%wide.region_5.9_spmd.clone.sunk | while | flops 127552640 | bytes 4989037 | solution.py:89
  252.6 1.3 constant_dynamic-slice_fusion.7
  255.1 1.3 constant_dynamic-slice_fusion.7
  257.7 1.3 constant_dynamic-slice_fusion.7
  260.2 1.3 constant_dynamic-slice_fusion.7
  262.8 1.3 constant_dynamic-slice_fusion.7
  265.3 1.3 constant_dynamic-slice_fusion.7
  267.8 1.3 constant_dynamic-slice_fusion.7
  270.4 1.3 constant_dynamic-slice_fusion.7
  273.9 8.1 %reshape_reshape_reshape.6 = bf16[256,40,256]{2,1,0:T(8,128)(2,1)} reshape(bf16[128,20480]{1,0:T(8,128)(2,1)} %get-tuple-element.229) | data formatting | bytes 10485760 | tf_op jit(solution)/shard_map/reshape;reshape;reshape | solution.py:148
  282.0 8.1 %reshape_reshape_reshape.7 = bf16[256,40,256]{2,1,0:T(8,128)(2,1)} reshape(bf16[128,20480]{1,0:T(8,128)(2,1)} %get-tuple-element.228) | data formatting | bytes 10485760 | tf_op jit(solution)/shard_map/reshape;reshape;reshape | solution.py:151
  290.1 5.7 %gather_fusion = bf16[256,40,256]{2,1,0:T(8,128)(2,1)} fusion(bf16[256,40,256]{2,1,0:T(8,128)(2,1)} %reshape_reshape_reshape.6, s32[1024]{0:T(1024)S(1)} %pad_clamp_fusion), kind=kCustom, calls=%fused_computation.clone | custom fusion | bytes 10486784 | tf_op jit(solution)/shard_map/jit(_take)/gather | solution.py:147
  295.8 5.8 %gather_fusion.1 = bf16[256,40,256]{2,1,0:T(8,128)(2,1)} fusion(bf16[256,40,256]{2,1,0:T(8,128)(2,1)} %reshape_reshape_reshape.7, s32[1024]{0:T(1024)S(1)} %pad_clamp_fusion), kind=kCustom, calls=%fused_computation.1.clone | custom fusion | bytes 10486784 | tf_op jit(solution)/shard_map/jit(_take)/gather | solution.py:150
  301.6 9.3 %broadcast_select_fusion = (bf16[256,40,256]{2,1,0:T(8,128)(2,1)}, bf16[256,40,256]{2,1,0:T(8,128)(2,1)}) fusion(bf16[256,40,256]{2,1,0:T(8,128)(2,1)} %gather_fusion.1, pred[256]{0:T(512)(128)(4,1)S(1)} %compare_and_fusion, bf16[256,40,256]{2,1,0:T(8,128)(2,1)} %gather_fusion), kind=kLoop, calls=%fused_computation.43 | loop fusion | flops 5242880 | bytes 20971776 | tf_op jit(solution)/shard_map/jit(_take)/select_n | solution.py:150
  310.9 8.3 %reshape_reshape.7 = bf16[32,320,2,128]{3,2,1,0:T(2,128)(2,1)} reshape(bf16[256,40,256]{2,1,0:T(8,128)(2,1)} %get-tuple-element.239) | data formatting | bytes 10485760 | tf_op jit(solution)/shard_map/reshape;reshape | solution.py:82
  319.2 8.4 %reshape_reshape.8 = bf16[32,320,2,128]{3,2,1,0:T(2,128)(2,1)} reshape(bf16[256,40,256]{2,1,0:T(8,128)(2,1)} %get-tuple-element.238) | data formatting | bytes 10485760 | tf_op jit(solution)/shard_map/reshape;reshape | solution.py:83
  327.6 88.5 %while.30 = (s32[]{:T(128)}, f32[2,4,80]{2,1,0:T(4,128)S(1)}, f32[2,4,80]{2,1,0:T(4,128)S(1)}, f32[2,4,80,128]{3,2,1,0:T(8,128)S(1)}, s32[32,320]{1,0:T(8,128)S(...) while((s32[]{:T(128)}, f32[2,4,80]{2,1,0:T(4,128)S(1)}, ...), condition=%wide.region_4.6_spmd.clone, body=%wide.region_1.5_spmd.clone.sunk | while | flops 106975440 | bytes 4408457 | solution.py:99
  327.9 1.2 constant_dynamic-slice_fusion.6
  330.7 1.2 constant_dynamic-slice_fusion.6
  333.4 1.2 constant_dynamic-slice_fusion.6
  336.2 1.2 constant_dynamic-slice_fusion.6
  339.0 1.2 constant_dynamic-slice_fusion.6
  347.3 1.2 constant_dynamic-slice_fusion.6
  350.0 1.2 constant_dynamic-slice_fusion.6
  352.8 1.2 constant_dynamic-slice_fusion.6
  358.3 1.2 constant_dynamic-slice_fusion.6
  361.1 1.2 constant_dynamic-slice_fusion.6
  363.8 1.2 constant_dynamic-slice_fusion.6
  366.6 1.2 constant_dynamic-slice_fusion.6
  372.1 1.2 constant_dynamic-slice_fusion.6
  374.9 1.2 constant_dynamic-slice_fusion.6
  377.7 1.2 constant_dynamic-slice_fusion.6
  380.4 1.2 constant_dynamic-slice_fusion.6
  386.0 1.2 constant_dynamic-slice_fusion.6
  388.7 1.2 constant_dynamic-slice_fusion.6
  391.5 1.2 constant_dynamic-slice_fusion.6
  399.8 1.2 constant_dynamic-slice_fusion.6
  402.6 1.2 constant_dynamic-slice_fusion.6
  405.3 1.2 constant_dynamic-slice_fusion.6
  410.9 1.2 constant_dynamic-slice_fusion.6
  413.6 1.2 constant_dynamic-slice_fusion.6
  (417 shorter events, 77.3 us)
Async XLA Ops:
  7.2 208.3 %all-gather.3.cloned.1.call-start = ((), (), s32[]{:S(2)}) async-start(), calls=%async_computation | async-start | bytes 13737984 | tf_op jit(solution)/shard_map/all_gather | solution.py:22
  319.2 8.4 %copy-start = (f32[2,4,80,128]{3,2,1,0:T(8,128)S(1)}, f32[2,4,80,128]{3,2,1,0:T(8,128)}, u32[]{:S(2)}) copy-start(f32[2,4,80,128]{3,2,1,0:T(8,128)} %custom-call.2) | copy-start | bytes 983044
Sparse Core Ops, SparseCore 0:
  12.7 202.7 all-gather.2
where the time goes:
time: 426 us; the launch traced here: 424 us
  waiting for transfers between devices  198 us (46%)
  local copies, waits for them, and re-layouts  142 us (33%)
  other arithmetic  35.3 us (8%)
  matrix products  31.7 us (7%)
  between operations  14.3 us (3%)
    all_gather x1, waiting for transfers between devices, one_gather(): lines, at, finished = (lax.all_gather(line, axis), 0, [])  198 us
    dynamic_slice x64, local copies, waits for them, and re-layouts, sweep_keys(): lax.scan(masked_step, carry_state, (key_blocks, value_blocks, place_blocks))  40.1 us
    all_gather x1, local copies, waits for them, and re-layouts, one_gather(): lines, at, finished = (lax.all_gather(line, axis), 0, [])  17.8 us
    dot_general x40, matrix products, update_rows(): jnp.einsum('qkgd,rkd->kgqr', queries, key_rows, preferred_element_type=jn...  16.7 us
    reduce_sum x40, other arithmetic, update_rows(): weight_sum = weight_sum * factor + jnp.sum(weights, -1)  15.7 us
    dot_general x40, matrix products, update_rows(): jnp.einsum('kgqr,rkd->kgqd', weights.astype(jnp.bfloat16), value_rows, pr...  15 us
    another operation x2, local copies, waits for them, and re-layouts, sweep_keys(): key_rows.reshape((block_count, block_rows) + key_rows.shape[1:])  13.2 us
    slice x2, local copies, waits for them, and re-layouts, one_gather(): pieces = lines[:, at:at + a.size].reshape(-1, *a.shape)  12.4 us
  transfers between devices with their start and end apart: 1, of which 1 were waited for; matrix products, arithmetic and copies ran while one was open for 1% of the time, Pallas kernels for 0%

commit v1 on v0

v1 whole, which is shorter than its diff:
```python
import jax
import jax.numpy as jnp
import numpy as np
from jax import lax
from jax.experimental import pallas as pl
from jax.experimental.pallas import tpu as pltpu
from jax.sharding import PartitionSpec as P

HEAD_DIM = 128
HEADS = 16
KV_HEADS = 4
GROUP = HEADS // KV_HEADS
RING = 8
STEP_DEVICES = 4
NEG_FILL = -1e30
LOG2E = 1.4426950408889634

BF16 = jnp.bfloat16
F32 = jnp.float32


def rows_of(*pieces):
    return jnp.concatenate(pieces, 0)


def frequencies():
    lane = np.arange(HEAD_DIM) % (HEAD_DIM // 2)
    return (500000.0 ** (-(lane * 2.0) / HEAD_DIM)).astype(np.float32)[None, :]


def prepare_kernel(order, freq, sq, sk, sv, cq, ck, cv, q_out, kv_out):
    me = lax.axis_index("context")
    rows = sq.shape[0]
    span = rows // 2
    first, second = order[2 * me], order[2 * me + 1]
    swap = first > second
    early, late = jnp.minimum(first, second), jnp.maximum(first, second)
    row = lax.broadcasted_iota(jnp.int32, (rows, HEAD_DIM), 0)
    lane = lax.broadcasted_iota(jnp.int32, (rows, HEAD_DIM), 1)
    place = jnp.where(row < span, early * span + row, late * span + row - span)
    angle = place.astype(F32) * freq[...]
    cosine = jnp.cos(angle)
    sine = jnp.sin(angle)
    sine = jnp.where(lane < HEAD_DIM // 2, -sine, sine)

    def ordered(ref, head):
        x = ref[:, head * HEAD_DIM : (head + 1) * HEAD_DIM].astype(F32)
        return jnp.where(swap, rows_of(x[span:], x[:span]), x)

    def rotated(ref, head):
        x = ordered(ref, head)
        return x * cosine + pltpu.roll(x, HEAD_DIM // 2, 1) * sine

    def plain(ref, head):
        return ref[:, head * HEAD_DIM : (head + 1) * HEAD_DIM].astype(F32)

    heads = sq.shape[1] // HEAD_DIM
    copies = q_out.shape[0] // heads
    for head in range(heads):
        block = rows_of(rotated(sq, head), plain(cq, head)).astype(BF16)
        for c in range(copies):
            q_out[head * copies + c] = block
    for kv in range(heads // GROUP):
        block = rows_of(
            rotated(sk, kv), ordered(sv, kv), plain(ck, kv), plain(cv, kv)
        ).astype(BF16)
        for g in range(GROUP):
            kv_out[kv * GROUP + g] = block


def attend_kernel(
    subsets, order, q_in, kv_in, out, key_e, key_l, val_e, val_l, key_c, val_c, pos_e, pos_l
):
    step = pl.program_id(0)
    me = lax.axis_index("context")
    column = me % RING
    subset = (me // RING) % subsets
    rows = q_in.shape[1] // 2
    span = rows // 2
    image = kv_in.shape[1] // 2 - rows
    key_devices = kv_in.shape[0]
    per_column = key_devices // RING

    def spans_of(device):
        first, second = order[2 * device], order[2 * device + 1]
        return jnp.minimum(first, second), jnp.maximum(first, second)

    @pl.when(step == 0)
    def _():
        def pair(i, carry):
            a = kv_in[2 * i].astype(F32)
            b = kv_in[2 * i + 1].astype(F32)

            def put(ref, lo, hi):
                size = 2 * (hi - lo)
                at = pl.multiple_of(i * size, size)
                ref[pl.ds(at, size), :] = rows_of(a[lo:hi], b[lo:hi]).astype(BF16)

            put(key_e, 0, span)
            put(key_l, span, rows)
            put(val_e, rows, rows + span)
            put(val_l, rows + span, 2 * rows)
            put(key_c, 2 * rows, 2 * rows + image)
            put(val_c, 2 * rows + image, 2 * rows + 2 * image)
            return carry

        lax.fori_loop(0, key_devices // 2, pair, 0)
        lane = lax.broadcasted_iota(jnp.int32, pos_e.shape, 1)
        place_e, place_l = lane, lane
        for d in range(key_devices):
            device = ((d % per_column) * subsets + subset) * RING + d // per_column
            early, late = spans_of(device)
            here = lane >= d * span
            place_e = jnp.where(here, lane + (early - d) * span, place_e)
            place_l = jnp.where(here, lane + (late - d) * span, place_l)
        pos_e[...] = place_e
        pos_l[...] = place_l

    scale = HEAD_DIM ** (-0.5) * LOG2E
    blocks = [q_in[i].astype(F32) for i in range(STEP_DEVICES)]
    q_e = rows_of(*[b[:span] for b in blocks]).astype(BF16)
    q_l = rows_of(*[b[span:rows] for b in blocks]).astype(BF16)
    q_c = rows_of(*[b[rows:] for b in blocks]).astype(BF16)
    size = STEP_DEVICES * span
    row = lax.broadcasted_iota(jnp.int32, (size, 1), 0)
    place_e, place_l = row, row
    for i in range(STEP_DEVICES):
        early, late = spans_of((step * STEP_DEVICES + i) * RING + column)
        here = row >= i * span
        place_e = jnp.where(here, row + (early - i) * span, place_e)
        place_l = jnp.where(here, row + (late - i) * span, place_l)

    def scores(q, key):
        return lax.dot_general(
            q, key[...], (((1,), (1,)), ((), ())), preferred_element_type=F32
        )

    def finish(parts):
        peak = parts[0][0].max(-1, keepdims=True)
        for s, _ in parts[1:]:
            peak = jnp.maximum(peak, s.max(-1, keepdims=True))
        shift = jnp.maximum(peak, 0.1 * NEG_FILL)
        total, mixed = 0.0, 0.0
        for s, val in parts:
            w = jnp.exp2((s - shift) * scale)
            total = total + w.sum(-1, keepdims=True)
            mixed = mixed + jnp.dot(w.astype(BF16), val[...], preferred_element_type=F32)
        some = total > 0.0
        safe = jnp.where(some, total, 1.0)
        level = jnp.where(some, shift * scale + jnp.log2(safe), NEG_FILL)
        return mixed / safe, level

    def masked(s, key_places, query_places):
        return jnp.where(key_places[...] <= query_places, s, NEG_FILL)

    out_l, level_l = finish(
        [
            (scores(q_l, key_e), val_e),
            (masked(scores(q_l, key_l), pos_l, place_l), val_l),
        ]
    )
    out_e, level_e = finish([(masked(scores(q_e, key_e), pos_e, place_e), val_e)])
    out_c, level_c = finish([(scores(q_c, key_c), val_c)])

    lane = lax.broadcasted_iota(jnp.int32, (HEAD_DIM, HEAD_DIM), 1)
    for i in range(STEP_DEVICES):

        def mine(a, n):
            return a[i * n : (i + 1) * n]

        level = rows_of(mine(level_e, span), mine(level_l, span), mine(level_c, rows))
        table = jnp.zeros((HEAD_DIM, HEAD_DIM), F32)
        for c, chunk in enumerate((level[:HEAD_DIM], level[2 * rows - HEAD_DIM :])):
            for piece in range(3):
                part = chunk.astype(BF16).astype(F32)
                table = jnp.where(lane == 3 * c + piece, part, table)
                chunk = chunk - part
        out[i] = rows_of(
            mine(out_e, span), mine(out_l, span), mine(out_c, rows), table.T[:8]
        ).astype(BF16)


def combine_kernel(subsets, order, parts, self_out, cross_out):
    me = lax.axis_index("context")
    rows = self_out.shape[0]
    span = rows // 2
    swap = order[2 * me] > order[2 * me + 1]
    heads = parts.shape[0] // subsets
    levels = []
    for s in range(parts.shape[0]):
        t = parts[s, 2 * rows : 2 * rows + 8, :].astype(F32)
        levels.append((t[0:1] + t[1:2] + t[2:3], t[3:4] + t[4:5] + t[5:6]))
    shares = [[], []]
    for head in range(heads):
        for c in range(2):
            own = [levels[head * subsets + p][c] for p in range(subsets)]
            peak = own[0]
            for level in own[1:]:
                peak = jnp.maximum(peak, level)
            weights = [jnp.exp2(level - peak) for level in own]
            total = weights[0]
            for w in weights[1:]:
                total = total + w
            shares[c] += [w / total for w in weights]
    count = 2 * parts.shape[0]
    table = rows_of(*shares[0], *shares[1], jnp.zeros((HEAD_DIM - count, HEAD_DIM), F32)).T
    for head in range(heads):
        mixed = 0.0
        for p in range(subsets):
            s = head * subsets + p
            again = 2 * HEAD_DIM - 2 * rows
            other = parts.shape[0] + s
            share = rows_of(table[:, s : s + 1], table[again:, other : other + 1])
            mixed = mixed + share * parts[s, : 2 * rows, :].astype(F32)
        columns = slice(head * HEAD_DIM, (head + 1) * HEAD_DIM)
        first, second = mixed[:span], mixed[span:rows]
        self_out[:, columns] = jnp.where(
            swap, rows_of(second, first), rows_of(first, second)
        ).astype(BF16)
        cross_out[:, columns] = mixed[rows:].astype(BF16)


def whole(memory=pltpu.VMEM):
    return pl.BlockSpec(memory_space=memory)


def body(self_queries, self_keys, self_values, cross_queries, cross_keys, cross_values, span_order):
    context = lax.axis_size("context")
    rows = self_queries.shape[0]
    image = cross_keys.shape[0]
    heads = self_queries.shape[1] // HEAD_DIM
    height = context // RING
    subsets = height // heads
    columns = [[z * RING + x for z in range(height)] for x in range(RING)]
    subset_columns = [c[p::subsets] for c in columns for p in range(subsets)]
    lines = [[z * RING + x for x in range(RING)] for z in range(height)]
    key_devices = RING * heads
    kv_rows = 2 * (rows + image)

    queries, keys = pl.pallas_call(
        prepare_kernel,
        in_specs=[whole(pltpu.SMEM)] + [whole()] * 7,
        out_specs=[whole(), whole()],
        out_shape=[
            jax.ShapeDtypeStruct((height, 2 * rows, HEAD_DIM), BF16),
            jax.ShapeDtypeStruct((heads, kv_rows, HEAD_DIM), BF16),
        ],
        name="prepare",
    )(
        span_order,
        jnp.asarray(frequencies()),
        self_queries,
        self_keys,
        self_values,
        cross_queries,
        cross_keys,
        cross_values,
    )
    keys = lax.all_to_all(keys, "context", 0, 0, axis_index_groups=subset_columns)
    keys = lax.all_gather(keys, "context", axis_index_groups=lines)
    queries = lax.all_to_all(queries, "context", 0, 0, axis_index_groups=columns)

    out_rows = 2 * rows + 8
    span_keys = key_devices * rows // 2
    partial_out = pl.pallas_call(
        lambda *refs: attend_kernel(subsets, *refs),
        grid=(height // STEP_DEVICES,),
        in_specs=[
            whole(pltpu.SMEM),
            pl.BlockSpec((STEP_DEVICES, 2 * rows, HEAD_DIM), lambda i: (i, 0, 0)),
            pl.BlockSpec((key_devices, kv_rows, HEAD_DIM), lambda i: (0, 0, 0)),
        ],
        out_specs=pl.BlockSpec((STEP_DEVICES, out_rows, HEAD_DIM), lambda i: (i, 0, 0)),
        out_shape=jax.ShapeDtypeStruct((height, out_rows, HEAD_DIM), BF16),
        scratch_shapes=[pltpu.VMEM((span_keys, HEAD_DIM), BF16)] * 4
        + [pltpu.VMEM((key_devices * image, HEAD_DIM), BF16)] * 2
        + [pltpu.VMEM((1, span_keys), jnp.int32)] * 2,
        compiler_params=pltpu.CompilerParams(
            dimension_semantics=("arbitrary",), vmem_limit_bytes=56 * 1024 * 1024
        ),
        name="attend",
    )(span_order, queries, keys.reshape(key_devices, kv_rows, HEAD_DIM))
    partial_out = lax.all_to_all(partial_out, "context", 0, 0, axis_index_groups=columns)

    return tuple(
        pl.pallas_call(
            lambda *refs: combine_kernel(subsets, *refs),
            in_specs=[whole(pltpu.SMEM), whole()],
            out_specs=[whole(), whole()],
            out_shape=[jax.ShapeDtypeStruct((rows, heads * HEAD_DIM), BF16)] * 2,
            name="combine",
        )(span_order, partial_out)
    )


def solution(mesh):
    rows = P(("groups", "context"), "tensor")
    return jax.shard_map(
        body,
        mesh=mesh,
        in_specs=(rows,) * 6 + (P("groups"),),
        out_specs=(rows, rows),
        check_vma=False,
    )
```

time: 426 us -> 207 us (0.49)
  waiting for transfers between devices: 198 us -> 12.2 us
  blocking collectives: 0 us -> 153 us
  local copies, waits for them, and re-layouts: 142 us -> 0 us
  other arithmetic: 35.3 us -> 0 us
  matrix products: 31.7 us -> 0 us
  Pallas kernels: 0 us -> 24.5 us
    all_gather x1, waiting for transfers between devices: 198 us -> 12.2 us  [body(): keys = lax.all_gather(keys, 'context', axis_index_groups=lines)]
    all_to_all x0 -> x3, blocking collectives: none -> 153 us  [the longest x1 62.1 us: body(): lax.all_to_all(keys, 'context', 0, 0, axis_index_groups=subset_columns)]
    dynamic_slice x72 -> x0, local copies, waits for them, and re-layouts: 50.5 us -> none  [the longest x64 40.1 us: sweep_keys(): lax.scan(masked_step, carry_state, (key_blocks, value_blocks, place_blocks))]
    another operation x6 -> x0, local copies, waits for them, and re-layouts: 39.8 us -> none  [the longest x2 13.2 us: sweep_keys(): key_rows.reshape((block_count, block_rows) + key_rows.shape[1:])]
    dot_general x80 -> x0, matrix products: 31.7 us -> none  [the longest x40 16.7 us: update_rows(): jnp.einsum('qkgd,rkd->kgqr', queries, key_rows, preferred_element_type=jn...]
    pallas_call x0 -> x3, Pallas kernels: none -> 24.5 us  [the longest x1 19.7 us: body(): pl.pallas_call(lambda *refs: attend_kernel(subsets, *refs), grid=(height...]
    all_gather x1 -> x0, local copies, waits for them, and re-layouts: 17.8 us -> none  [one_gather(): lines, at, finished = (lax.all_gather(line, axis), 0, [])]
    reduce_sum x40 -> x0, other arithmetic: 15.7 us -> none  [update_rows(): weight_sum = weight_sum * factor + jnp.sum(weights, -1)]
  transfers between devices with their start and end apart: 1 -> 1, of which waited for: 1 -> 1; matrix products, arithmetic and copies ran while one was open for 1% -> 0% of each run, Pallas kernels for 0% -> 0%
where the time goes in v1:
time: 207 us; the launch traced here: 204 us
  blocking collectives  153 us (74%)
  Pallas kernels  24.5 us (12%)
  between operations  14.1 us (7%)
  waiting for transfers between devices  12.2 us (6%)
    all_to_all x1, blocking collectives, body(): lax.all_to_all(keys, 'context', 0, 0, axis_index_groups=subset_columns)  62.1 us
    all_to_all x1, blocking collectives, body(): lax.all_to_all(partial_out, 'context', 0, 0, axis_index_groups=columns)  46.8 us
    all_to_all x1, blocking collectives, body(): lax.all_to_all(queries, 'context', 0, 0, axis_index_groups=columns)  43.8 us
    pallas_call x1, Pallas kernels, body(): pl.pallas_call(lambda *refs: attend_kernel(subsets, *refs), grid=(height...  19.7 us
    all_gather x1, waiting for transfers between devices, body(): keys = lax.all_gather(keys, 'context', axis_index_groups=lines)  12.2 us
  transfers between devices with their start and end apart: 1, of which 1 were waited for; matrix products, arithmetic and copies ran while one was open for 0% of the time, Pallas kernels for 0%

profile of v1, /device:TPU:65, one launch (start us, length us, event | category | flops | bytes accessed | tf_op | source)
XLA Modules:
  0.0 203.6 jit_solution(7390509491752943577)
XLA Ops:
  7.2 0.1 all-gather.3.cloned.1.call-start
  7.2 2.4 %prepare.1 = (bf16[16,160,128]{2,1,0:T(8,128)(2,1)}, bf16[8,208,128]{2,1,0:T(8,128)(2,1)}) custom-call(s32[256]{0:T(256)} %refs_0_.3, f32[1,128]{1,0:T(1,128)} %constant.2.clone.freq, bf16[80,1024]{1,0:T(8,128)(2,1)} %sq.1, bf16[80,256]{1,0:T(8,128)(2,1)} %sk.1, bf16[80,256]{1,0:T(8,128)(2,1)} %sv.1, bf16[80,1024]{1,0:T(8,128)(2,1)} %cq.1, ...), custom_call_target="tpu_custom_call" | custom-call | tf_op jit(solution)/shard_map/prepare/pallas_call | solution.py:240
  9.6 62.1 %all_to_all.15 = bf16[8,208,128]{2,1,0:T(8,128)(2,1)} all-to-all(bf16[8,208,128]{2,1,0:T(8,128)(2,1)} %get-tuple-element.5), channel_id=1, replica_groups={{0,32,64,96,128,160,192,224},{16,48,80,112,144,176,208,240},{2,34,66,98..., dimensions={0} | all-to-all | bytes 851968 | tf_op jit(solution)/shard_map/all_to_all | solution.py:259
  71.8 0.1 all-gather.3.cloned.1.call-update
  71.8 43.8 %all_to_all.16.refs_1_ = bf16[16,160,128]{2,1,0:T(8,128)(2,1)} all-to-all(bf16[16,160,128]{2,1,0:T(8,128)(2,1)} %get-tuple-element.4), channel_id=1, replica_groups={{0,16,32,48,64,80,96,112,128,144,160,176,192,208,224,240},{2,18,34,50,6..., dimensions={0} | all-to-all | bytes 1310720 | tf_op jit(solution)/shard_map/all_to_all | solution.py:261
  115.6 12.2 %all-gather.3.cloned.1.call-done.refs_2_ = bf16[64,208,128]{2,1,0:T(8,128)(2,1)} async-done(((bf16[8,208,128]{2,1,0:T(8,128)(2,1)}), bf16[64,208,128]{2,1,0:T(8,128)(2,1)}) %all-gather.3.cloned.1.call-update) | async-done | bytes 3407888 | tf_op jit(solution)/shard_map/all_gather | solution.py:260
  127.8 19.7 %attend.1 = bf16[16,168,128]{2,1,0:T(8,128)(2,1)} custom-call(s32[256]{0:T(256)} %refs_0_.3, bf16[16,160,128]{2,1,0:T(8,128)(2,1)} %all_to_all.16.refs_1_, bf16[64,208,128]{2,1,0:T(8,128)(2,1)} %all-gather.3.cloned.1.call-done.refs_2_), custom_call_target="tpu_custom_call" | custom-call | tf_op jit(solution)/shard_map/attend/pallas_call | solution.py:265
  147.5 46.8 %all_to_all.17.refs_1_ = bf16[16,168,128]{2,1,0:T(8,128)(2,1)} all-to-all(bf16[16,168,128]{2,1,0:T(8,128)(2,1)} %attend.1), channel_id=1, replica_groups={{0,16,32,48,64,80,96,112,128,144,160,176,192,208,224,240},{2,18,34,50,6..., dimensions={0} | all-to-all | bytes 1376256 | tf_op jit(solution)/shard_map/all_to_all | solution.py:283
  194.3 2.4 %combine.1 = (bf16[80,1024]{1,0:T(8,128)(2,1)}, bf16[80,1024]{1,0:T(8,128)(2,1)}) custom-call(s32[256]{0:T(256)} %refs_0_.3, bf16[16,168,128]{2,1,0:T(8,128)(2,1)} %all_to_all.17.refs_1_), custom_call_target="tpu_custom_call" | custom-call | tf_op jit(solution)/shard_map/combine/pallas_call | solution.py:286
Async XLA Ops:
  7.2 120.6 %all-gather.3.cloned.1.call-start = ((), (), s32[]{:S(2)}) async-start(), calls=%async_computation.3 | async-start | bytes 3833856 | tf_op jit(solution)/shard_map/all_gather | solution.py:260
Sparse Core Ops, SparseCore 0:
  72.0 55.7 all-gather.2

commit v2 on v1

v2 whole, which is shorter than its diff:
```python
import jax
import jax.numpy as jnp
import numpy as np
from jax import lax
from jax.experimental import pallas as pl
from jax.experimental.pallas import tpu as pltpu
from jax.sharding import PartitionSpec as P

HEAD_DIM = 128
HEADS = 16
KV_HEADS = 4
GROUP = HEADS // KV_HEADS
RING = 8
PAIR = 2
PIECES = 3
NEG_FILL = -1e30
LOG2E = 1.4426950408889634

BF16 = jnp.bfloat16
F32 = jnp.float32


def rows_of(*pieces):
    return jnp.concatenate(pieces, 0)


def frequencies():
    lane = np.arange(HEAD_DIM) % (HEAD_DIM // 2)
    return (500000.0 ** (-(lane * 2.0) / HEAD_DIM)).astype(np.float32)[None, :]


def prepare_kernel(order, freq, sq, sk, sv, cq, ck, cv, q_out, kv_out):
    me = lax.axis_index("context")
    rows = sq.shape[0]
    span = rows // 2
    first, second = order[2 * me], order[2 * me + 1]
    swap = first > second
    early, late = jnp.minimum(first, second), jnp.maximum(first, second)
    row = lax.broadcasted_iota(jnp.int32, (rows, HEAD_DIM), 0)
    lane = lax.broadcasted_iota(jnp.int32, (rows, HEAD_DIM), 1)
    place = jnp.where(row < span, early * span + row, late * span + row - span)
    angle = place.astype(F32) * freq[...]
    cosine = jnp.cos(angle)
    sine = jnp.sin(angle)
    sine = jnp.where(lane < HEAD_DIM // 2, -sine, sine)

    def ordered(ref, head):
        x = ref[:, head * HEAD_DIM : (head + 1) * HEAD_DIM].astype(F32)
        return jnp.where(swap, rows_of(x[span:], x[:span]), x)

    def rotated(ref, head):
        x = ordered(ref, head)
        return x * cosine + pltpu.roll(x, HEAD_DIM // 2, 1) * sine

    def plain(ref, head):
        return ref[:, head * HEAD_DIM : (head + 1) * HEAD_DIM].astype(F32)

    kv_local = sk.shape[1] // HEAD_DIM
    for kv in range(kv_local):
        block = rows_of(
            rotated(sk, kv), ordered(sv, kv), plain(ck, kv), plain(cv, kv)
        ).astype(BF16)
        for m in range(kv, kv_out.shape[0], kv_local):
            kv_out[m] = block
    for kv in range(kv_local):
        heads = range(kv * GROUP, (kv + 1) * GROUP)
        turned = [rotated(sq, head) for head in heads]
        block = rows_of(
            *[x[:span] for x in turned],
            *[x[span:] for x in turned],
            *[plain(cq, head) for head in heads],
        ).astype(BF16)
        for m in range(kv, q_out.shape[0], kv_local):
            q_out[m] = block


def spans_of(order, device):
    first, second = order[2 * device], order[2 * device + 1]
    return jnp.minimum(first, second), jnp.maximum(first, second)


def scores(q, key):
    return lax.dot_general(q, key[...], (((1,), (1,)), ((), ())), preferred_element_type=F32)


def finish(parts):
    scale = HEAD_DIM ** (-0.5) * LOG2E
    peak = parts[0][0].max(-1, keepdims=True)
    for s, _ in parts[1:]:
        peak = jnp.maximum(peak, s.max(-1, keepdims=True))
    shift = jnp.maximum(peak, 0.1 * NEG_FILL)
    total, mixed = 0.0, 0.0
    for s, val in parts:
        w = jnp.exp2((s - shift) * scale)
        total = total + w.sum(-1, keepdims=True)
        mixed = mixed + jnp.dot(w.astype(BF16), val[...], preferred_element_type=F32)
    some = total > 0.0
    safe = jnp.where(some, total, 1.0)
    level = jnp.where(some, shift * scale + jnp.log2(safe), NEG_FILL)
    return mixed / safe, level


def chunks_of(size):
    return [min(at, size - HEAD_DIM) for at in range(0, size, HEAD_DIM)]


def stat_rows(size):
    return -(-PIECES * len(chunks_of(size)) // 16) * 16


def with_levels(mixed, level):
    lane = lax.broadcasted_iota(jnp.int32, (HEAD_DIM, HEAD_DIM), 1)
    table = jnp.zeros((HEAD_DIM, HEAD_DIM), F32)
    for c, at in enumerate(chunks_of(level.shape[0])):
        rest = level[at : at + HEAD_DIM]
        for piece in range(PIECES):
            part = rest.astype(BF16).astype(F32)
            table = jnp.where(lane == PIECES * c + piece, part, table)
            rest = rest - part
    return rows_of(mixed, table.T[: stat_rows(level.shape[0])]).astype(BF16)


def gathered_rows(kv_in, targets):
    def pair(i, carry):
        a = kv_in[2 * i].astype(F32)
        b = kv_in[2 * i + 1].astype(F32)
        for ref, lo, hi in targets:
            size = 2 * (hi - lo)
            at = pl.multiple_of(i * size, size)
            ref[pl.ds(at, size), :] = rows_of(a[lo:hi], b[lo:hi]).astype(BF16)
        return carry

    lax.fori_loop(0, kv_in.shape[0] // 2, pair, 0)


def cross_kernel(rows, q_in, kv_in, out, key, val):
    image = kv_in.shape[1] // 2 - rows

    @pl.when(pl.program_id(0) == 0)
    def _():
        low = 2 * rows
        gathered_rows(kv_in, [(key, low, low + image), (val, low + image, low + 2 * image)])

    out[0] = with_levels(*finish([(scores(q_in[0], key), val)]))


def self_kernel(rows, order, q_in, kv_in, out, key_e, key_l, val_e, val_l, pos_e, pos_l):
    step = pl.program_id(0)
    me = lax.axis_index("context")
    span = rows // 2

    @pl.when(step == 0)
    def _():
        gathered_rows(
            kv_in,
            [
                (key_e, 0, span),
                (key_l, span, rows),
                (val_e, rows, rows + span),
                (val_l, rows + span, 2 * rows),
            ],
        )
        pair = me % RING // PAIR
        lane = lax.broadcasted_iota(jnp.int32, pos_e.shape, 1)
        place_e, place_l = lane, lane
        for d in range(kv_in.shape[0]):
            line, column = d // PAIR, pair * PAIR + d % PAIR
            early, late = spans_of(order, line * RING + column)
            here = lane >= d * span
            place_e = jnp.where(here, lane + (early - d) * span, place_e)
            place_l = jnp.where(here, lane + (late - d) * span, place_l)
        pos_e[...] = place_e
        pos_l[...] = place_l

    size = GROUP * span
    early, late = spans_of(order, me // RING * RING + step)
    within = lax.broadcasted_iota(jnp.int32, (size, 1), 0) % span

    def masked(s, key_places, query_places):
        return jnp.where(key_places[...] <= query_places, s, NEG_FILL)

    q_e, q_l = q_in[0, :size], q_in[0, size:]
    out_e, level_e = finish([(masked(scores(q_e, key_e), pos_e, early * span + within), val_e)])
    out_l, level_l = finish(
        [
            (scores(q_l, key_e), val_e),
            (masked(scores(q_l, key_l), pos_l, late * span + within), val_l),
        ]
    )
    out[0] = with_levels(rows_of(out_e, out_l), rows_of(level_e, level_l))


def combine_kernel(order, self_parts, cross_parts, self_out, cross_out):
    me = lax.axis_index("context")
    rows = self_out.shape[0]
    span = rows // 2
    swap = order[2 * me] > order[2 * me + 1]
    kv_local = self_out.shape[1] // (HEAD_DIM * GROUP)
    subsets = self_parts.shape[0] // kv_local
    size = GROUP * rows
    starts = chunks_of(size)

    def mix(parts):
        shares = [[None] * len(starts) for _ in range(parts.shape[0])]
        for kv in range(kv_local):
            members = [j * kv_local + kv for j in range(subsets)]
            stats = [parts[s, size:, :].astype(F32) for s in members]
            for c in range(len(starts)):
                own = []
                for t in stats:
                    level = t[PIECES * c : PIECES * c + 1]
                    for piece in range(1, PIECES):
                        level = level + t[PIECES * c + piece : PIECES * c + piece + 1]
                    own.append(level)
                peak = own[0]
                for level in own[1:]:
                    peak = jnp.maximum(peak, level)
                weights = [jnp.exp2(level - peak) for level in own]
                total = weights[0]
                for w in weights[1:]:
                    total = total + w
                for s, w in zip(members, weights):
                    shares[s][c] = w / total
        flat = [w for share in shares for w in share]
        table = rows_of(*flat, jnp.zeros((HEAD_DIM - len(flat), HEAD_DIM), F32)).T
        results = []
        for kv in range(kv_local):
            mixed = 0.0
            for j in range(subsets):
                s = j * kv_local + kv
                pieces, done = [], 0
                for c, at in enumerate(starts):
                    column = s * len(starts) + c
                    pieces.append(table[done - at :, column : column + 1])
                    done = at + HEAD_DIM
                mixed = mixed + rows_of(*pieces) * parts[s, :size, :].astype(F32)
            results.append(mixed)
        return results

    for kv, mixed in enumerate(mix(self_parts)):
        for g in range(GROUP):
            head = kv * GROUP + g
            early = mixed[g * span : (g + 1) * span]
            late = mixed[(GROUP + g) * span : (GROUP + g + 1) * span]
            self_out[:, head * HEAD_DIM : (head + 1) * HEAD_DIM] = jnp.where(
                swap, rows_of(late, early), rows_of(early, late)
            ).astype(BF16)
    for kv, mixed in enumerate(mix(cross_parts)):
        for g in range(GROUP):
            head = kv * GROUP + g
            cross_out[:, head * HEAD_DIM : (head + 1) * HEAD_DIM] = mixed[
                g * rows : (g + 1) * rows
            ].astype(BF16)


def whole(memory=pltpu.VMEM):
    return pl.BlockSpec(memory_space=memory)


def body(self_queries, self_keys, self_values, cross_queries, cross_keys, cross_values, span_order):
    context = lax.axis_size("context")
    rows = self_queries.shape[0]
    image = cross_keys.shape[0]
    heads = self_queries.shape[1] // HEAD_DIM
    height = context // RING
    lines = [[z * RING + x for x in range(RING)] for z in range(height)]
    squares = [
        [(z + a) * RING + x + b for a in range(PAIR) for b in range(PAIR)]
        for z in range(0, height, PAIR)
        for x in range(0, RING, PAIR)
    ]
    columns = [
        [z * RING + x for z in range(p, height, PAIR)] for p in range(PAIR) for x in range(RING)
    ]
    key_devices = height * PAIR
    kv_rows = 2 * (rows + image)
    size = GROUP * rows

    queries, keys = pl.pallas_call(
        prepare_kernel,
        in_specs=[whole(pltpu.SMEM)] + [whole()] * 7,
        out_specs=[whole(), whole()],
        out_shape=[
            jax.ShapeDtypeStruct((RING, 2 * size, HEAD_DIM), BF16),
            jax.ShapeDtypeStruct((PAIR * PAIR, kv_rows, HEAD_DIM), BF16),
        ],
        name="prepare",
    )(
        span_order,
        jnp.asarray(frequencies()),
        self_queries,
        self_keys,
        self_values,
        cross_queries,
        cross_keys,
        cross_values,
    )
    keys = lax.all_to_all(keys, "context", 0, 0, axis_index_groups=squares)
    keys = lax.all_gather(keys, "context", axis_index_groups=columns)
    queries = lax.all_to_all(queries, "context", 0, 0, axis_index_groups=lines)
    keys = keys.reshape(key_devices, kv_rows, HEAD_DIM)

    out_rows = size + stat_rows(size)

    def attend(kernel, half, order, scratch, name):
        return pl.pallas_call(
            lambda *refs: kernel(rows, *refs),
            grid=(RING,),
            in_specs=[whole(pltpu.SMEM)] * len(order)
            + [
                pl.BlockSpec((1, size, HEAD_DIM), lambda i: (i, half, 0)),
                pl.BlockSpec((key_devices, kv_rows, HEAD_DIM), lambda i: (0, 0, 0)),
            ],
            out_specs=pl.BlockSpec((1, out_rows, HEAD_DIM), lambda i: (i, 0, 0)),
            out_shape=jax.ShapeDtypeStruct((RING, out_rows, HEAD_DIM), BF16),
            scratch_shapes=scratch,
            compiler_params=pltpu.CompilerParams(
                dimension_semantics=("arbitrary",), vmem_limit_bytes=48 * 1024 * 1024
            ),
            cost_estimate=pl.CostEstimate(
                flops=4 * RING * size * HEAD_DIM * key_devices * rows,
                transcendentals=RING * size * key_devices * rows,
                bytes_accessed=2 * key_devices * kv_rows * HEAD_DIM,
            ),
            name=name,
        )(*order, queries, keys)

    span_keys = key_devices * rows // 2
    image_keys = key_devices * image
    cross_parts = attend(
        cross_kernel, 1, (), [pltpu.VMEM((image_keys, HEAD_DIM), BF16)] * 2, "cross"
    )
    cross_parts = lax.all_to_all(cross_parts, "context", 0, 0, axis_index_groups=lines)
    self_parts = attend(
        self_kernel,
        0,
        (span_order,),
        [pltpu.VMEM((span_keys, HEAD_DIM), BF16)] * 4 + [pltpu.VMEM((1, span_keys), jnp.int32)] * 2,
        "self",
    )
    self_parts = lax.all_to_all(self_parts, "context", 0, 0, axis_index_groups=lines)

    return tuple(
        pl.pallas_call(
            combine_kernel,
            in_specs=[whole(pltpu.SMEM), whole(), whole()],
            out_specs=[whole(), whole()],
            out_shape=[jax.ShapeDtypeStruct((rows, heads * HEAD_DIM), BF16)] * 2,
            name="combine",
        )(span_order, self_parts, cross_parts)
    )


def solution(mesh):
    rows = P(("groups", "context"), "tensor")
    return jax.shard_map(
        body,
        mesh=mesh,
        in_specs=(rows,) * 6 + (P("groups"),),
        out_specs=(rows, rows),
        check_vma=False,
    )
```

time: 207 us -> 181 us (0.87)
  the two profiles are of different devices: /device:TPU:65 before, /device:TPU:192 now
where the time goes in v2:
time: 181 us
  blocking collectives  95 us (52%)
  waiting for transfers between devices  34.4 us (19%)
  Pallas kernels  26.9 us (15%)
  between operations  14.1 us (8%)
  starting transfers between devices  7.65 us (4%)
  local copies, waits for them, and re-layouts  2.91 us (2%)
    all_to_all x1, blocking collectives, body(): keys = lax.all_to_all(keys, 'context', 0, 0, axis_index_groups=squares)  46.4 us
    all_gather x1, waiting for transfers between devices, body(): keys = lax.all_gather(keys, 'context', axis_index_groups=columns)  29.1 us
    all_to_all x1, blocking collectives, body(): queries = lax.all_to_all(queries, 'context', 0, 0, axis_index_groups=lines)  25.2 us
    all_to_all x1, blocking collectives, body(): lax.all_to_all(self_parts, 'context', 0, 0, axis_index_groups=lines)  23.4 us
    pallas_call x2, Pallas kernels, attend(): pl.pallas_call(lambda *refs: kernel(rows, *refs), grid=(RING,), in_specs=...  21 us
    all_to_all x1, starting transfers between devices, body(): lax.all_to_all(cross_parts, 'context', 0, 0, axis_index_groups=lines)  7.58 us
    all_to_all x1, waiting for transfers between devices, body(): lax.all_to_all(cross_parts, 'context', 0, 0, axis_index_groups=lines)  5.24 us
  transfers between devices with their start and end apart: 2, of which 2 were waited for; matrix products, arithmetic and copies ran while one was open for 0% of the time, Pallas kernels for 8%

profile of v2, /device:TPU:192, one launch (start us, length us, event | category | flops | bytes accessed | tf_op | source)
XLA Modules:
  0.0 181.0 jit_solution(15952709724752768857)
XLA Ops:
  7.2 0.1 all-gather.3.cloned.1.call-start
  7.2 2.6 %prepare.1 = (bf16[8,640,128]{2,1,0:T(8,128)(2,1)}, bf16[4,208,128]{2,1,0:T(8,128)(2,1)}) custom-call(s32[256]{0:T(256)} %order.3, f32[1,128]{1,0:T(1,128)} %constant.2.clone.freq, bf16[80,1024]{1,0:T(8,128)(2,1)} %sq.1, bf16[80,256]{1,0:T(8,128)(2,1)} %sk.1, bf16[80,256]{1,0:T(8,128)(2,1)} %sv.1, bf16[80,1024]{1,0:T(8,128)(2,1)} %cq.1, bf16[24,256]{1,0:T(8,128)(2,1)} %ck.1, ...), custom_call_target="tpu_custom_call" | custom-call | tf_op jit(solution)/shard_map/prepare/pallas_call | solution.py:279
  9.8 46.4 %all_to_all.20 = bf16[4,208,128]{2,1,0:T(8,128)(2,1)} all-to-all(bf16[4,208,128]{2,1,0:T(8,128)(2,1)} %get-tuple-element.5), channel_id=1, replica_groups={{0,2,16,18},{4,6,20,22},{8,10,24,26},{12,14,28,30},{32,34,48,50},{36,38..., dimensions={0} | all-to-all | bytes 425984 | tf_op jit(solution)/shard_map/all_to_all | solution.py:298
  56.2 0.1 all-gather.3.cloned.1.call-update
  56.2 25.2 %all_to_all.21.refs_1_.refs_0_ = bf16[8,640,128]{2,1,0:T(8,128)(2,1)S(1)} all-to-all(bf16[8,640,128]{2,1,0:T(8,128)(2,1)} %get-tuple-element.4), channel_id=1, replica_groups={{0,2,4,6,8,10,12,14},{16,18,20,22,24,26,28,30},{32,34,36,38,40,42,44,46..., dimensions={0} | all-to-all | bytes 2621440 | tf_op jit(solution)/shard_map/all_to_all | solution.py:300
  81.5 29.1 %all-gather.3.cloned.1.call-done.refs_2_.refs_1_ = bf16[32,208,128]{2,1,0:T(8,128)(2,1)} async-done(((bf16[4,208,128]{2,1,0:T(8,128)(2,1)}), bf16[32,208,128]{2,1,0:T(8,128)(2,1)}) %all-gather.3.cloned.1.call-update) | async-done | bytes 1703952 | tf_op jit(solution)/shard_map/all_gather | solution.py:299
  110.6 0.0 copy-start.1
  110.6 1.5 copy-done.1
  112.0 7.4 %cross.1 = bf16[8,336,128]{2,1,0:T(8,128)(2,1)} custom-call(bf16[8,640,128]{2,1,0:T(8,128)(2,1)S(1)} %all_to_all.21.refs_1_.refs_0_, bf16[32,208,128]{2,1,0:T(8,128)(2,1)S(1)} %copy-done.1), custom_call_target="tpu_custom_call" | custom-call | flops 3355443200 | bytes 1703936 | tf_op jit(solution)/shard_map/cross/pallas_call | solution.py:306
  119.4 0.0 copy-start
  119.4 7.6 %all-to-all-start.3 = ((bf16[8,336,128]{2,1,0:T(8,128)(2,1)}), bf16[8,336,128]{2,1,0:T(8,128)(2,1)S(1)}, u32[]{:S(2)}, u32[]{:S(2)}) async-start(bf16[8,336,128]{2,1,0:T(8,128)(2,1)} %cross.1), calls=%async_computation.3 | async-start | bytes 1376256 | tf_op jit(solution)/shard_map/all_to_all | solution.py:333
  127.0 0.0 copy-done
  127.0 0.0 copy-start.2
  127.0 1.4 copy-done.2
  128.5 13.6 %self.1 = bf16[8,336,128]{2,1,0:T(8,128)(2,1)S(1)} custom-call(s32[256]{0:T(256)S(1)} %copy-done, bf16[8,640,128]{2,1,0:T(8,128)(2,1)S(1)} %all_to_all.21.refs_1_.refs_0_, bf16[32,208,128]{2,1,0:T(8,128)(2,1)S(1)} %copy-done.2), custom_call_target="tpu_custom_call" | custom-call | flops 3355443200 | bytes 1703936 | tf_op jit(solution)/shard_map/self/pallas_call | solution.py:306
  142.1 5.2 %all-to-all-done.3.cross_parts = bf16[8,336,128]{2,1,0:T(8,128)(2,1)S(1)} async-done(((bf16[8,336,128]{2,1,0:T(8,128)(2,1)}), bf16[8,336,128]{2,1,0:T(8,128)(2,1)S(1)}, u32[]{:S(2)}, u32[]{:S(2)}) %all-to-all-start.3) | async-done | bytes 688160 | tf_op jit(solution)/shard_map/all_to_all | solution.py:333
  147.3 0.0 copy-start.3
  147.3 23.4 %all_to_all.22.self_parts = bf16[8,336,128]{2,1,0:T(8,128)(2,1)} all-to-all(bf16[8,336,128]{2,1,0:T(8,128)(2,1)S(1)} %self.1), channel_id=1, replica_groups={{0,2,4,6,8,10,12,14},{16,18,20,22,24,26,28,30},{32,34,36,38,40,42,44,46..., dimensions={0} | all-to-all | bytes 1376256 | tf_op jit(solution)/shard_map/all_to_all | solution.py:341
  170.8 0.0 copy-done.3
  170.8 3.3 %combine.1 = (bf16[80,1024]{1,0:T(8,128)(2,1)}, bf16[80,1024]{1,0:T(8,128)(2,1)}) custom-call(s32[256]{0:T(256)} %order.3, bf16[8,336,128]{2,1,0:T(8,128)(2,1)} %all_to_all.22.self_parts, bf16[8,336,128]{2,1,0:T(8,128)(2,1)} %copy-done.3), custom_call_target="tpu_custom_call" | custom-call | tf_op jit(solution)/shard_map/combine/pallas_call | solution.py:344
Async XLA Ops:
  7.2 103.4 %all-gather.3.cloned.1.call-start = ((), (), s32[]{:S(2)}) async-start(), calls=%async_computation.4 | async-start | bytes 1916928 | tf_op jit(solution)/shard_map/all_gather | solution.py:299
  110.6 1.5 copy-start.1
  119.4 7.6 %copy-start = (s32[256]{0:T(256)S(1)}, s32[256]{0:T(256)}, u32[]{:S(2)}) copy-start(s32[256]{0:T(256)} %order.3) | copy-start | bytes 3076
  119.4 27.9 %all-to-all-start.3 = ((bf16[8,336,128]{2,1,0:T(8,128)(2,1)}), bf16[8,336,128]{2,1,0:T(8,128)(2,1)S(1)}, u32[]{:S(2)}, u32[]{:S(2)}) async-start(bf16[8,336,128]{2,1,0:T(8,128)(2,1)} %cross.1), calls=%async_computation.3 | async-start | bytes 1376256 | tf_op jit(solution)/shard_map/all_to_all | solution.py:333
  127.0 1.5 copy-start.2
  147.3 23.4 %copy-start.3 = (bf16[8,336,128]{2,1,0:T(8,128)(2,1)}, bf16[8,336,128]{2,1,0:T(8,128)(2,1)S(1)}, u32[]{:S(2)}) copy-start(bf16[8,336,128]{2,1,0:T(8,128)(2,1)S(1)} %all-to-all-done.3.cross_parts) | copy-start | bytes 2064388
Sparse Core Ops, SparseCore 0:
  56.4 54.1 all-gather.2

commit v3 on v2

v3 whole, which is shorter than its diff:
```python
import jax
import jax.numpy as jnp
import numpy as np
from jax import lax
from jax.experimental import pallas as pl
from jax.experimental.pallas import tpu as pltpu
from jax.sharding import PartitionSpec as P


HEAD_DIM = 128
HEADS = 16
KV_HEADS = 4
GROUP = HEADS // KV_HEADS
RING = 8
HALF = RING // 2
PAIR = 2
STEP = 4
PIECES = 3
NEG_FILL = -1e30
LOG2E = 1.4426950408889634

BF16 = jnp.bfloat16
F32 = jnp.float32


def rows_of(*pieces):
    return jnp.concatenate(pieces, 0)


def frequencies():
    lane = np.arange(HEAD_DIM) % (HEAD_DIM // 2)
    return (500000.0 ** (-(lane * 2.0) / HEAD_DIM)).astype(np.float32)[None, :]


def spans_of(order, device):
    first, second = order[2 * device], order[2 * device + 1]
    return jnp.minimum(first, second), jnp.maximum(first, second)


def local_order(order, freq, rows):
    me = lax.axis_index("context")
    span = rows // 2
    swap = order[2 * me] > order[2 * me + 1]
    early, late = spans_of(order, me)
    row = lax.broadcasted_iota(jnp.int32, (rows, HEAD_DIM), 0)
    lane = lax.broadcasted_iota(jnp.int32, (rows, HEAD_DIM), 1)
    place = jnp.where(row < span, early * span + row, late * span + row - span)
    angle = place.astype(F32) * freq[...]
    cosine = jnp.cos(angle)
    sine = jnp.sin(angle)
    sine = jnp.where(lane < HEAD_DIM // 2, -sine, sine)

    def ordered(ref, head):
        x = plain(ref, head)
        return jnp.where(swap, rows_of(x[span:], x[:span]), x)

    def rotated(ref, head):
        x = ordered(ref, head)
        return x * cosine + pltpu.roll(x, HEAD_DIM // 2, 1) * sine

    return ordered, rotated


def plain(ref, head):
    return ref[:, head * HEAD_DIM : (head + 1) * HEAD_DIM].astype(F32)


def prepare_kernel(order, freq, sq, sk, sv, cq, ck, cv, q_out, kv_out):
    rows = sq.shape[0]
    span = rows // 2
    ordered, rotated = local_order(order, freq, rows)
    kv_local = sk.shape[1] // HEAD_DIM
    for kv in range(kv_local):
        block = rows_of(
            rotated(sk, kv), ordered(sv, kv), plain(ck, kv), plain(cv, kv)
        ).astype(BF16)
        for m in range(kv, kv_out.shape[0], kv_local):
            kv_out[m] = block
    for kv in range(kv_local):
        heads = range(kv * GROUP, (kv + 1) * GROUP)
        turned = [rotated(sq, head) for head in heads]
        block = rows_of(
            *[x[:span] for x in turned],
            *[x[span:] for x in turned],
            *[plain(cq, head) for head in heads],
        ).astype(BF16)
        for m in range(kv, q_out.shape[0], kv_local):
            q_out[m] = block


def scores(q, key):
    return lax.dot_general(q, key[...], (((1,), (1,)), ((), ())), preferred_element_type=F32)


def peak_of(parts):
    peak = parts[0].max(-1, keepdims=True)
    for s in parts[1:]:
        peak = jnp.maximum(peak, s.max(-1, keepdims=True))
    return jnp.maximum(peak, 0.1 * NEG_FILL)


def finish(parts):
    scale = HEAD_DIM ** (-0.5) * LOG2E
    shift = peak_of([s for s, _ in parts])
    total, mixed = 0.0, 0.0
    for s, val in parts:
        w = jnp.exp2((s - shift) * scale)
        total = total + w.sum(-1, keepdims=True)
        mixed = mixed + jnp.dot(w.astype(BF16), val[...], preferred_element_type=F32)
    some = total > 0.0
    safe = jnp.where(some, total, 1.0)
    level = jnp.where(some, shift * scale + jnp.log2(safe), NEG_FILL)
    return mixed * (1.0 / safe), level


def chunks_of(size):
    return [min(at, size - HEAD_DIM) for at in range(0, size, HEAD_DIM)]


def stat_rows(size):
    return -(-PIECES * len(chunks_of(size)) // 16) * 16


def with_levels(mixed, level):
    lane = lax.broadcasted_iota(jnp.int32, (HEAD_DIM, HEAD_DIM), 1)
    table = jnp.zeros((HEAD_DIM, HEAD_DIM), F32)
    for c, at in enumerate(chunks_of(level.shape[0])):
        rest = level[at : at + HEAD_DIM]
        for piece in range(PIECES):
            part = rest.astype(BF16).astype(F32)
            table = jnp.where(lane == PIECES * c + piece, part, table)
            rest = rest - part
    return rows_of(mixed, table.T[: stat_rows(level.shape[0])]).astype(BF16)


def gathered_rows(kv_in, targets):
    def pair(i, carry):
        a = kv_in[2 * i].astype(F32)
        b = kv_in[2 * i + 1].astype(F32)
        for ref, lo, hi in targets:
            size = 2 * (hi - lo)
            at = pl.multiple_of(i * size, size)
            ref[pl.ds(at, size), :] = rows_of(a[lo:hi], b[lo:hi]).astype(BF16)
        return carry

    lax.fori_loop(0, kv_in.shape[0] // 2, pair, 0)


def cross_kernel(rows, q_in, kv_hbm, out, kv_in, key, val, sem):
    image = kv_in.shape[1] // 2

    @pl.when(pl.program_id(0) == 0)
    def _():
        copy = pltpu.make_async_copy(kv_hbm.at[:, 2 * rows : 2 * rows + 2 * image, :], kv_in, sem)
        copy.start()
        copy.wait()
        gathered_rows(kv_in, [(key, 0, image), (val, image, 2 * image)])

    s = [scores(q_in[i], key) for i in range(STEP)]
    for i in range(STEP):
        out[i] = with_levels(*finish([(s[i], val)]))


def self_kernel(rows, order, q_in, kv_in, out, key_e, key_l, val_e, val_l, pos_e, pos_l):
    step = pl.program_id(0)
    me = lax.axis_index("context")
    line, column = me // RING, me % RING
    span = rows // 2

    @pl.when(step == 0)
    def _():
        gathered_rows(
            kv_in,
            [
                (key_e, 0, span),
                (key_l, span, rows),
                (val_e, rows, rows + span),
                (val_l, rows + span, 2 * rows),
            ],
        )
        low = line % PAIR * RING + column % HALF // PAIR * PAIR
        lane = lax.broadcasted_iota(jnp.int32, pos_e.shape, 1)
        place_e, place_l = lane, lane
        for d in range(kv_in.shape[0]):
            b = d % (PAIR * PAIR)
            device = low + d // (PAIR * PAIR) * PAIR * RING + b // PAIR * HALF + b % PAIR
            early, late = spans_of(order, device)
            here = lane >= d * span
            place_e = jnp.where(here, lane + (early - d) * span, place_e)
            place_l = jnp.where(here, lane + (late - d) * span, place_l)
        pos_e[...] = place_e
        pos_l[...] = place_l

    size = GROUP * span
    within = lax.broadcasted_iota(jnp.int32, (size, 1), 0) % span
    base = line // PAIR * PAIR * RING + column // HALF * HALF

    def masked(s, key_places, query_places):
        return jnp.where(key_places[...] <= query_places, s, NEG_FILL)

    s_ee, s_le, s_ll, ends = [], [], [], []
    for i in range(STEP):
        source = step * STEP + i
        ends.append(spans_of(order, base + source // HALF * RING + source % HALF))
        q_e, q_l = q_in[i, :size], q_in[i, size:]
        s_ee.append(scores(q_e, key_e))
        s_le.append(scores(q_l, key_e))
        s_ll.append(scores(q_l, key_l))
    for i in range(STEP):
        early, late = ends[i]
        out_e, level_e = finish([(masked(s_ee[i], pos_e, early * span + within), val_e)])
        out_l, level_l = finish(
            [(s_le[i], val_e), (masked(s_ll[i], pos_l, late * span + within), val_l)]
        )
        out[i] = with_levels(rows_of(out_e, out_l), rows_of(level_e, level_l))


def mix(parts, size, kv_local):
    starts = chunks_of(size)
    subsets = parts.shape[0] // kv_local
    shares = [[None] * len(starts) for _ in range(parts.shape[0])]
    for kv in range(kv_local):
        members = [j * kv_local + kv for j in range(subsets)]
        stats = [parts[s, size:, :].astype(F32) for s in members]
        for c in range(len(starts)):
            own = []
            for t in stats:
                level = t[PIECES * c : PIECES * c + 1]
                for piece in range(1, PIECES):
                    level = level + t[PIECES * c + piece : PIECES * c + piece + 1]
                own.append(level)
            peak = own[0]
            for level in own[1:]:
                peak = jnp.maximum(peak, level)
            weights = [jnp.exp2(level - peak) for level in own]
            total = weights[0]
            for w in weights[1:]:
                total = total + w
            for s, w in zip(members, weights):
                shares[s][c] = w / total
    flat = [w for share in shares for w in share]
    table = rows_of(*flat, jnp.zeros((HEAD_DIM - len(flat), HEAD_DIM), F32)).T
    results = []
    for kv in range(kv_local):
        mixed = 0.0
        for j in range(subsets):
            s = j * kv_local + kv
            pieces, done = [], 0
            for c, at in enumerate(starts):
                column = s * len(starts) + c
                pieces.append(table[done - at :, column : column + 1])
                done = at + HEAD_DIM
            mixed = mixed + rows_of(*pieces) * parts[s, :size, :].astype(F32)
        results.append(mixed)
    return results


def self_combine_kernel(order, parts, out):
    me = lax.axis_index("context")
    rows = out.shape[0]
    span = rows // 2
    swap = order[2 * me] > order[2 * me + 1]
    kv_local = out.shape[1] // (HEAD_DIM * GROUP)
    for kv, mixed in enumerate(mix(parts, GROUP * rows, kv_local)):
        for g in range(GROUP):
            head = kv * GROUP + g
            early = mixed[g * span : (g + 1) * span]
            late = mixed[(GROUP + g) * span : (GROUP + g + 1) * span]
            out[:, head * HEAD_DIM : (head + 1) * HEAD_DIM] = jnp.where(
                swap, rows_of(late, early), rows_of(early, late)
            ).astype(BF16)


def cross_combine_kernel(parts, out):
    rows = out.shape[0]
    kv_local = out.shape[1] // (HEAD_DIM * GROUP)
    for kv, mixed in enumerate(mix(parts, GROUP * rows, kv_local)):
        for g in range(GROUP):
            head = kv * GROUP + g
            out[:, head * HEAD_DIM : (head + 1) * HEAD_DIM] = mixed[
                g * rows : (g + 1) * rows
            ].astype(BF16)


def whole(memory=pltpu.VMEM):
    return pl.BlockSpec(memory_space=memory)


def attention(self_queries, self_keys, self_values, cross_queries, cross_keys, cross_values, span_order):
    context = lax.axis_size("context")
    rows = self_queries.shape[0]
    image = cross_keys.shape[0]
    heads = self_queries.shape[1] // HEAD_DIM
    height = context // RING
    patches = [
        [(z + a) * RING + x + b for a in range(PAIR) for b in range(HALF)]
        for z in range(0, height, PAIR)
        for x in range(0, RING, HALF)
    ]
    quads = [
        [z * RING + x + HALF * a + b for a in range(PAIR) for b in range(PAIR)]
        for z in range(height)
        for x in range(0, HALF, PAIR)
    ]
    columns = [
        [z * RING + x for z in range(p, height, PAIR)] for p in range(PAIR) for x in range(RING)
    ]
    key_devices = height * PAIR
    kv_rows = 2 * (rows + image)
    size = GROUP * rows

    queries, keys = pl.pallas_call(
        prepare_kernel,
        in_specs=[whole(pltpu.SMEM)] + [whole()] * 7,
        out_specs=[whole(), whole()],
        out_shape=[
            jax.ShapeDtypeStruct((RING, 2 * size, HEAD_DIM), BF16),
            jax.ShapeDtypeStruct((PAIR * PAIR, kv_rows, HEAD_DIM), BF16),
        ],
        name="prepare",
    )(
        span_order,
        jnp.asarray(frequencies()),
        self_queries,
        self_keys,
        self_values,
        cross_queries,
        cross_keys,
        cross_values,
    )
    keys = lax.all_to_all(keys, "context", 0, 0, axis_index_groups=quads)
    keys = lax.all_gather(keys, "context", axis_index_groups=columns)
    queries = lax.all_to_all(queries, "context", 0, 0, axis_index_groups=patches)
    keys = keys.reshape(key_devices, kv_rows, HEAD_DIM)

    out_rows = size + stat_rows(size)

    def attend(kernel, half, queries, order, kv_spec, scratch):
        return pl.pallas_call(
            lambda *refs: kernel(rows, *refs),
            grid=(RING // STEP,),
            in_specs=[whole(pltpu.SMEM)] * len(order)
            + [
                pl.BlockSpec((STEP, size, HEAD_DIM), lambda i: (i, half, 0)),
                kv_spec,
            ],
            out_specs=pl.BlockSpec((STEP, out_rows, HEAD_DIM), lambda i: (i, 0, 0)),
            out_shape=jax.ShapeDtypeStruct((RING, out_rows, HEAD_DIM), BF16),
            scratch_shapes=scratch,
            compiler_params=pltpu.CompilerParams(
                dimension_semantics=("arbitrary",), vmem_limit_bytes=48 * 1024 * 1024
            ),
            cost_estimate=pl.CostEstimate(
                flops=4 * RING * size * HEAD_DIM * key_devices * rows,
                transcendentals=RING * size * key_devices * rows,
                bytes_accessed=2 * key_devices * kv_rows * HEAD_DIM,
            ),
        )(*order, queries, keys)

    span_keys = key_devices * rows // 2
    image_keys = key_devices * image
    cross_parts = attend(
        cross_kernel,
        1,
        queries,
        (),
        whole(pl.ANY),
        [pltpu.VMEM((key_devices, 2 * image, HEAD_DIM), BF16)]
        + [pltpu.VMEM((image_keys, HEAD_DIM), BF16)] * 2
        + [pltpu.SemaphoreType.DMA],
    )
    cross_parts = lax.all_to_all(cross_parts, "context", 0, 0, axis_index_groups=patches)
    self_parts = attend(
        self_kernel,
        0,
        queries,
        (span_order,),
        pl.BlockSpec((key_devices, kv_rows, HEAD_DIM), lambda i: (0, 0, 0)),
        [pltpu.VMEM((span_keys, HEAD_DIM), BF16)] * 4 + [pltpu.VMEM((1, span_keys), jnp.int32)] * 2,
    )
    self_parts = lax.all_to_all(self_parts, "context", 0, 0, axis_index_groups=patches)
    out_shape = jax.ShapeDtypeStruct((rows, heads * HEAD_DIM), BF16)
    cross_out = pl.pallas_call(
        cross_combine_kernel,
        in_specs=[whole()],
        out_specs=whole(),
        out_shape=out_shape,
        name="cross_combine",
    )(cross_parts)
    self_out = pl.pallas_call(
        self_combine_kernel,
        in_specs=[whole(pltpu.SMEM), whole()],
        out_specs=whole(),
        out_shape=out_shape,
        name="self_combine",
    )(span_order, self_parts)
    return self_out, cross_out


def solution(mesh):
    rows = P(("groups", "context"), "tensor")
    return jax.shard_map(
        attention,
        mesh=mesh,
        in_specs=(rows,) * 6 + (P("groups"),),
        out_specs=(rows, rows),
        check_vma=False,
    )
```

time: 181 us -> 185 us (1.022)
  the two profiles are of different devices: /device:TPU:192 before, /device:TPU:65 now
where the time goes in v3:
time: 185 us
  waiting for transfers between devices  114 us (62%)
  Pallas kernels  22.5 us (12%)
  starting transfers between devices  16.2 us (9%)
  blocking collectives  15.7 us (8%)
  between operations  14.1 us (8%)
  local copies, waits for them, and re-layouts  2.31 us (1%)
    all_gather x1, waiting for transfers between devices, attention(): keys = lax.all_gather(keys, 'context', axis_index_groups=columns)  92.2 us
    all_to_all x1, blocking collectives, attention(): keys = lax.all_to_all(keys, 'context', 0, 0, axis_index_groups=quads)  15.7 us
    pallas_call x2, Pallas kernels, attend(): pl.pallas_call(lambda *refs: kernel(rows, *refs), grid=(RING // STEP,), i...  15.2 us
    all_to_all x1, waiting for transfers between devices, attention(): lax.all_to_all(self_parts, 'context', 0, 0, axis_index_groups=patches)  14.6 us
    all_to_all x1, starting transfers between devices, attention(): lax.all_to_all(queries, 'context', 0, 0, axis_index_groups=patches)  7.96 us
    all_to_all x1, waiting for transfers between devices, attention(): lax.all_to_all(cross_parts, 'context', 0, 0, axis_index_groups=patches)  6.27 us
    all_to_all x1, starting transfers between devices, attention(): lax.all_to_all(cross_parts, 'context', 0, 0, axis_index_groups=patches)  4.4 us
    all_to_all x1, starting transfers between devices, attention(): lax.all_to_all(self_parts, 'context', 0, 0, axis_index_groups=patches)  3.75 us
  transfers between devices with their start and end apart: 4, of which 3 were waited for; matrix products, arithmetic and copies ran while one was open for 0% of the time, Pallas kernels for 7%

profile of v3, /device:TPU:65, one launch (start us, length us, event | category | flops | bytes accessed | tf_op | source)
XLA Modules:
  0.0 184.6 jit_solution(6011880961662875186)
XLA Ops:
  7.2 2.6 %prepare.1 = (bf16[8,640,128]{2,1,0:T(8,128)(2,1)}, bf16[4,208,128]{2,1,0:T(8,128)(2,1)}) custom-call(s32[256]{0:T(256)} %order.3, f32[1,128]{1,0:T(1,128)} %constant.2.clone.freq, bf16[80,1024]{1,0:T(8,128)(2,1)} %sq.1, bf16[80,256]{1,0:T(8,128)(2,1)} %sk.1, bf16[80,256]{1,0:T(8,128)(2,1)} %sv.1, bf16[80,1024]{1,0:T(8,128)(2,1)} %cq.1, bf16[24,256]{1,0:T(8,128)(2,1)} %ck.1, ...), custom_call_target="tpu_custom_call" | custom-call | tf_op jit(solution)/shard_map/prepare/pallas_call | solution.py:312
  9.7 15.7 %all_to_all.20 = bf16[4,208,128]{2,1,0:T(8,128)(2,1)} all-to-all(bf16[4,208,128]{2,1,0:T(8,128)(2,1)} %get-tuple-element.5), channel_id=1, replica_groups={{0,2,8,10},{4,6,12,14},{16,18,24,26},{20,22,28,30},{32,34,40,42},{36,38..., dimensions={0} | all-to-all | bytes 425984 | tf_op jit(solution)/shard_map/all_to_all | solution.py:331
  25.5 8.0 %all-to-all-start = ((bf16[8,640,128]{2,1,0:T(8,128)(2,1)}), bf16[8,640,128]{2,1,0:T(8,128)(2,1)S(1)}, u32[]{:S(2)}, u32[]{:S(2)}) async-start(bf16[8,640,128]{2,1,0:T(8,128)(2,1)} %get-tuple-element.4), calls=%async_computation | async-start | bytes 2621440 | tf_op jit(solution)/shard_map/all_to_all | solution.py:333
  33.4 0.1 all-gather.3.cloned.1.call-start
  33.5 0.7 all-gather.3.cloned.1.call-update
  34.2 92.2 %all-gather.3.cloned.1.call-done.refs_2_.refs_1_ = bf16[32,208,128]{2,1,0:T(8,128)(2,1)} async-done(((bf16[4,208,128]{2,1,0:T(8,128)(2,1)}), bf16[32,208,128]{2,1,0:T(8,128)(2,1)}) %all-gather.3.cloned.1.call-update) | async-done | bytes 1703952 | tf_op jit(solution)/shard_map/all_gather | solution.py:332
  126.4 0.0 all-to-all-done.refs_1_.refs_0_
  126.4 0.0 copy-start.1
  126.4 1.5 copy-done.1
  127.9 0.0 copy-start.2
  127.9 4.2 %shard_map.96 = bf16[8,336,128]{2,1,0:T(8,128)(2,1)} custom-call(bf16[8,640,128]{2,1,0:T(8,128)(2,1)S(1)} %all-to-all-done.refs_1_.refs_0_, bf16[32,208,128]{2,1,0:T(8,128)(2,1)S(1)} %copy-done.1), custom_call_target="tpu_custom_call" | custom-call | flops 3355443200 | bytes 1703936 | tf_op jit(solution)/shard_map/pallas_call | solution.py:339
  132.1 0.0 copy-start
  132.1 4.4 %all-to-all-start.3 = ((bf16[8,336,128]{2,1,0:T(8,128)(2,1)}), bf16[8,336,128]{2,1,0:T(8,128)(2,1)}, u32[]{:S(2)}, u32[]{:S(2)}) async-start(bf16[8,336,128]{2,1,0:T(8,128)(2,1)} %shard_map.96), calls=%async_computation.3 | async-start | bytes 1376256 | tf_op jit(solution)/shard_map/all_to_all | solution.py:372
  136.5 0.0 copy-done.2
  136.5 0.0 copy-done
  136.5 11.0 %shard_map.95 = bf16[8,336,128]{2,1,0:T(8,128)(2,1)} custom-call(s32[256]{0:T(256)S(1)} %copy-done, bf16[8,640,128]{2,1,0:T(8,128)(2,1)S(1)} %all-to-all-done.refs_1_.refs_0_, bf16[32,208,128]{2,1,0:T(8,128)(2,1)S(1)} %copy-done.2), custom_call_target="tpu_custom_call" | custom-call | flops 3355443200 | bytes 1703936 | tf_op jit(solution)/shard_map/pallas_call | solution.py:339
  147.5 6.3 %all-to-all-done.3.parts = bf16[8,336,128]{2,1,0:T(8,128)(2,1)} async-done(((bf16[8,336,128]{2,1,0:T(8,128)(2,1)}), bf16[8,336,128]{2,1,0:T(8,128)(2,1)}, u32[]{:S(2)}, u32[]{:S(2)}) %all-to-all-start.3) | async-done | bytes 688160 | tf_op jit(solution)/shard_map/all_to_all | solution.py:372
  153.8 3.7 %all-to-all-start.2 = ((bf16[8,336,128]{2,1,0:T(8,128)(2,1)}), bf16[8,336,128]{2,1,0:T(8,128)(2,1)S(1)}, u32[]{:S(2)}, u32[]{:S(2)}) async-start(bf16[8,336,128]{2,1,0:T(8,128)(2,1)} %shard_map.95), calls=%async_computation.2 | async-start | bytes 1376256 | tf_op jit(solution)/shard_map/all_to_all | solution.py:381
  157.6 2.4 %cross_combine.1 = bf16[80,1024]{1,0:T(8,128)(2,1)} custom-call(bf16[8,336,128]{2,1,0:T(8,128)(2,1)} %all-to-all-done.3.parts), custom_call_target="tpu_custom_call" | custom-call | tf_op jit(solution)/shard_map/cross_combine/pallas_call | solution.py:383
  159.9 14.6 %all-to-all-done.2.parts = bf16[8,336,128]{2,1,0:T(8,128)(2,1)S(1)} async-done(((bf16[8,336,128]{2,1,0:T(8,128)(2,1)}), bf16[8,336,128]{2,1,0:T(8,128)(2,1)S(1)}, u32[]{:S(2)}, u32[]{:S(2)}) %all-to-all-start.2) | async-done | bytes 688160 | tf_op jit(solution)/shard_map/all_to_all | solution.py:381
  174.5 0.0 copy-start.3
  174.5 0.8 copy-done.3
  175.4 2.4 %self_combine.1 = bf16[80,1024]{1,0:T(8,128)(2,1)} custom-call(s32[256]{0:T(256)} %order.3, bf16[8,336,128]{2,1,0:T(8,128)(2,1)} %copy-done.3), custom_call_target="tpu_custom_call" | custom-call | tf_op jit(solution)/shard_map/self_combine/pallas_call | solution.py:390
Async XLA Ops:
  25.5 101.0 %all-to-all-start = ((bf16[8,640,128]{2,1,0:T(8,128)(2,1)}), bf16[8,640,128]{2,1,0:T(8,128)(2,1)S(1)}, u32[]{:S(2)}, u32[]{:S(2)}) async-start(bf16[8,640,128]{2,1,0:T(8,128)(2,1)} %get-tuple-element.4), calls=%async_computation | async-start | bytes 2621440 | tf_op jit(solution)/shard_map/all_to_all | solution.py:333
  33.4 93.0 %all-gather.3.cloned.1.call-start = ((), (), s32[]{:S(2)}) async-start(), calls=%async_computation.4 | async-start | bytes 1916928 | tf_op jit(solution)/shard_map/all_gather | solution.py:332
  126.4 1.5 copy-start.1
  127.9 8.6 %copy-start.2 = (bf16[32,208,128]{2,1,0:T(8,128)(2,1)S(1)}, bf16[32,208,128]{2,1,0:T(8,128)(2,1)}, u32[]{:S(2)}) copy-start(bf16[32,208,128]{2,1,0:T(8,128)(2,1)} %all-gather.3.cloned.1.call-done.refs_2_.refs_1_) | copy-start | bytes 5111812
  132.1 4.4 %copy-start = (s32[256]{0:T(256)S(1)}, s32[256]{0:T(256)}, u32[]{:S(2)}) copy-start(s32[256]{0:T(256)} %order.3) | copy-start | bytes 3076
  132.1 21.7 %all-to-all-start.3 = ((bf16[8,336,128]{2,1,0:T(8,128)(2,1)}), bf16[8,336,128]{2,1,0:T(8,128)(2,1)}, u32[]{:S(2)}, u32[]{:S(2)}) async-start(bf16[8,336,128]{2,1,0:T(8,128)(2,1)} %shard_map.96), calls=%async_computation.3 | async-start | bytes 1376256 | tf_op jit(solution)/shard_map/all_to_all | solution.py:372
  153.8 20.7 %all-to-all-start.2 = ((bf16[8,336,128]{2,1,0:T(8,128)(2,1)}), bf16[8,336,128]{2,1,0:T(8,128)(2,1)S(1)}, u32[]{:S(2)}, u32[]{:S(2)}) async-start(bf16[8,336,128]{2,1,0:T(8,128)(2,1)} %shard_map.95), calls=%async_computation.2 | async-start | bytes 1376256 | tf_op jit(solution)/shard_map/all_to_all | solution.py:381
  174.5 0.9 copy-start.3
Sparse Core Ops, SparseCore 0:
  36.4 90.0 all-gather.2

commit v4 on v3

--- a/solution.py
+++ b/solution.py
@@ -12,10 +12,10 @@
 KV_HEADS = 4
 GROUP = HEADS // KV_HEADS
 RING = 8
-HALF = RING // 2
 PAIR = 2
+COPIES = 8
 STEP = 4
-PIECES = 3
+LEVEL_ROWS = 8
 NEG_FILL = -1e30
 LOG2E = 1.4426950408889634
 
@@ -113,27 +113,46 @@
     return mixed * (1.0 / safe), level
 
 
-def chunks_of(size):
-    return [min(at, size - HEAD_DIM) for at in range(0, size, HEAD_DIM)]
-
-
-def stat_rows(size):
-    return -(-PIECES * len(chunks_of(size)) // 16) * 16
-
-
 def with_levels(mixed, level):
+    half = HEAD_DIM // 2
+    columns, ends = [], level.shape[0] // HEAD_DIM * HEAD_DIM
+    for at in range(0, ends, HEAD_DIM):
+        columns += parts_of(level[at : at + HEAD_DIM])
+    first, second, third = parts_of(level[ends:])
+    columns += [rows_of(first, second), rows_of(third, jnp.zeros((half, 1), F32))]
     lane = lax.broadcasted_iota(jnp.int32, (HEAD_DIM, HEAD_DIM), 1)
     table = jnp.zeros((HEAD_DIM, HEAD_DIM), F32)
-    for c, at in enumerate(chunks_of(level.shape[0])):
-        rest = level[at : at + HEAD_DIM]
-        for piece in range(PIECES):
-            part = rest.astype(BF16).astype(F32)
-            table = jnp.where(lane == PIECES * c + piece, part, table)
-            rest = rest - part
-    return rows_of(mixed, table.T[: stat_rows(level.shape[0])]).astype(BF16)
-
-
-def gathered_rows(kv_in, targets):
+    for c, column in enumerate(columns):
+        table = jnp.where(lane == c, column, table)
+    return rows_of(mixed, table.T[:LEVEL_ROWS]).astype(BF16)
+
+
+def parts_of(level):
+    parts = []
+    for _ in range(3):
+        part = level.astype(BF16).astype(F32)
+        parts.append(part)
+        level = level - part
+    return parts
+
+
+def levels_of(rows):
+    whole_rows = [rows[c : c + 1] + rows[c + 1 : c + 2] + rows[c + 2 : c + 3] for c in (0, 3)]
+    return whole_rows + [rows[6:7] + pltpu.roll(rows[6:7], HEAD_DIM // 2, 1) + rows[7:8]]
+
+
+def gathered_rows(kv_hbm, low, kv_in, sems, targets):
+    chunk = kv_in.shape[0] // sems.shape[0]
+    rows = pl.ds(low, kv_in.shape[1])
+    copies = [
+        pltpu.make_async_copy(
+            kv_hbm.at[pl.ds(c * chunk, chunk), rows, :], kv_in.at[pl.ds(c * chunk, chunk)], sems.at[c]
+        )
+        for c in range(sems.shape[0])
+    ]
+    for copy in copies:
+        copy.start()
+
     def pair(i, carry):
         a = kv_in[2 * i].astype(F32)
         b = kv_in[2 * i + 1].astype(F32)
@@ -143,25 +162,27 @@
             ref[pl.ds(at, size), :] = rows_of(a[lo:hi], b[lo:hi]).astype(BF16)
         return carry
 
-    lax.fori_loop(0, kv_in.shape[0] // 2, pair, 0)
-
-
-def cross_kernel(rows, q_in, kv_hbm, out, kv_in, key, val, sem):
+    for c, copy in enumerate(copies):
+        copy.wait()
+        lax.fori_loop(c * chunk // 2, (c + 1) * chunk // 2, pair, 0)
+
+
+def cross_kernel(rows, q_in, kv_hbm, out, kv_in, key, val, sems):
     image = kv_in.shape[1] // 2
 
     @pl.when(pl.program_id(0) == 0)
     def _():
-        copy = pltpu.make_async_copy(kv_hbm.at[:, 2 * rows : 2 * rows + 2 * image, :], kv_in, sem)
-        copy.start()
-        copy.wait()
-        gathered_rows(kv_in, [(key, 0, image), (val, image, 2 * image)])
+        targets = [(key, 0, image), (val, image, 2 * image)]
+        gathered_rows(kv_hbm, 2 * rows, kv_in, sems, targets)
 
     s = [scores(q_in[i], key) for i in range(STEP)]
     for i in range(STEP):
         out[i] = with_levels(*finish([(s[i], val)]))
 
 
-def self_kernel(rows, order, q_in, kv_in, out, key_e, key_l, val_e, val_l, pos_e, pos_l):
+def self_kernel(
+    rows, order, q_in, kv_hbm, out, kv_in, key_e, key_l, val_e, val_l, pos_e, pos_l, sems
+):
     step = pl.program_id(0)
     me = lax.axis_index("context")
     line, column = me // RING, me % RING
@@ -170,7 +191,10 @@
     @pl.when(step == 0)
     def _():
         gathered_rows(
+            kv_hbm,
+            0,
             kv_in,
+            sems,
             [
                 (key_e, 0, span),
                 (key_l, span, rows),
@@ -178,13 +202,11 @@
                 (val_l, rows + span, 2 * rows),
             ],
         )
-        low = line % PAIR * RING + column % HALF // PAIR * PAIR
+        low = column // PAIR * PAIR
         lane = lax.broadcasted_iota(jnp.int32, pos_e.shape, 1)
         place_e, place_l = lane, lane
         for d in range(kv_in.shape[0]):
-            b = d % (PAIR * PAIR)
-            device = low + d // (PAIR * PAIR) * PAIR * RING + b // PAIR * HALF + b % PAIR
-            early, late = spans_of(order, device)
+            early, late = spans_of(order, d // PAIR * RING + low + d % PAIR)
             here = lane >= d * span
             place_e = jnp.where(here, lane + (early - d) * span, place_e)
             place_l = jnp.where(here, lane + (late - d) * span, place_l)
@@ -193,15 +215,13 @@
 
     size = GROUP * span
     within = lax.broadcasted_iota(jnp.int32, (size, 1), 0) % span
-    base = line // PAIR * PAIR * RING + column // HALF * HALF
 
     def masked(s, key_places, query_places):
         return jnp.where(key_places[...] <= query_places, s, NEG_FILL)
 
     s_ee, s_le, s_ll, ends = [], [], [], []
     for i in range(STEP):
-        source = step * STEP + i
-        ends.append(spans_of(order, base + source // HALF * RING + source % HALF))
+        ends.append(spans_of(order, line * RING + step * STEP + i))
         q_e, q_l = q_in[i, :size], q_in[i, size:]
         s_ee.append(scores(q_e, key_e))
         s_le.append(scores(q_l, key_e))
@@ -216,43 +236,25 @@
 
 
 def mix(parts, size, kv_local):
-    starts = chunks_of(size)
-    subsets = parts.shape[0] // kv_local
-    shares = [[None] * len(starts) for _ in range(parts.shape[0])]
+    count = parts.shape[0]
     for kv in range(kv_local):
-        members = [j * kv_local + kv for j in range(subsets)]
-        stats = [parts[s, size:, :].astype(F32) for s in members]
-        for c in range(len(starts)):
-            own = []
-            for t in stats:
-                level = t[PIECES * c : PIECES * c + 1]
-                for piece in range(1, PIECES):
-                    level = level + t[PIECES * c + piece : PIECES * c + piece + 1]
-                own.append(level)
-            peak = own[0]
-            for level in own[1:]:
-                peak = jnp.maximum(peak, level)
-            weights = [jnp.exp2(level - peak) for level in own]
-            total = weights[0]
-            for w in weights[1:]:
-                total = total + w
-            for s, w in zip(members, weights):
-                shares[s][c] = w / total
-    flat = [w for share in shares for w in share]
-    table = rows_of(*flat, jnp.zeros((HEAD_DIM - len(flat), HEAD_DIM), F32)).T
-    results = []
-    for kv in range(kv_local):
+        members = range(kv, count, kv_local)
+        levels = [levels_of(parts[s, size:, :].astype(F32)) for s in members]
+        peak = levels[0]
+        for level in levels[1:]:
+            peak = [jnp.maximum(a, b) for a, b in zip(peak, level)]
+        weights = [[jnp.exp2(a - b) for a, b in zip(level, peak)] for level in levels]
+        total = weights[0]
+        for weight in weights[1:]:
+            total = [a + b for a, b in zip(total, weight)]
+        flat = [a / b for weight in weights for a, b in zip(weight, total)]
+        per = len(total)
+        table = rows_of(*flat, jnp.zeros((HEAD_DIM - len(flat), HEAD_DIM), F32)).T
         mixed = 0.0
-        for j in range(subsets):
-            s = j * kv_local + kv
-            pieces, done = [], 0
-            for c, at in enumerate(starts):
-                column = s * len(starts) + c
-                pieces.append(table[done - at :, column : column + 1])
-                done = at + HEAD_DIM
-            mixed = mixed + rows_of(*pieces) * parts[s, :size, :].astype(F32)
-        results.append(mixed)
-    return results
+        for j, s in enumerate(members):
+            share = rows_of(*[table[:, j * per + c : j * per + c + 1] for c in range(per)])[:size]
+            mixed = mixed + share * parts[s, :size, :].astype(F32)
+        yield mixed
 
 
 def self_combine_kernel(order, parts, out):
@@ -292,15 +294,11 @@
     image = cross_keys.shape[0]
     heads = self_queries.shape[1] // HEAD_DIM
     height = context // RING
-    patches = [
-        [(z + a) * RING + x + b for a in range(PAIR) for b in range(HALF)]
+    lines = [[z * RING + x for x in range(RING)] for z in range(height)]
+    squares = [
+        [(z + a) * RING + x + b for a in range(PAIR) for b in range(PAIR)]
         for z in range(0, height, PAIR)
-        for x in range(0, RING, HALF)
-    ]
-    quads = [
-        [z * RING + x + HALF * a + b for a in range(PAIR) for b in range(PAIR)]
-        for z in range(height)
-        for x in range(0, HALF, PAIR)
+        for x in range(0, RING, PAIR)
     ]
     columns = [
         [z * RING + x for z in range(p, height, PAIR)] for p in range(PAIR) for x in range(RING)
@@ -328,12 +326,12 @@
         cross_keys,
         cross_values,
     )
-    keys = lax.all_to_all(keys, "context", 0, 0, axis_index_groups=quads)
+    keys = lax.all_to_all(keys, "context", 0, 0, axis_index_groups=squares)
     keys = lax.all_gather(keys, "context", axis_index_groups=columns)
-    queries = lax.all_to_all(queries, "context", 0, 0, axis_index_groups=patches)
+    queries = lax.all_to_all(queries, "context", 0, 0, axis_index_groups=lines)
     keys = keys.reshape(key_devices, kv_rows, HEAD_DIM)
 
-    out_rows = size + stat_rows(size)
+    out_rows = size + LEVEL_ROWS
 
     def attend(kernel, half, queries, order, kv_spec, scratch):
         return pl.pallas_call(
@@ -364,27 +362,32 @@
         1,
         queries,
         (),
-        whole(pl.ANY),
+        whole(pltpu.HBM),
         [pltpu.VMEM((key_devices, 2 * image, HEAD_DIM), BF16)]
         + [pltpu.VMEM((image_keys, HEAD_DIM), BF16)] * 2
-        + [pltpu.SemaphoreType.DMA],
+        + [pltpu.SemaphoreType.DMA((COPIES,))],
     )
-    cross_parts = lax.all_to_all(cross_parts, "context", 0, 0, axis_index_groups=patches)
+    cross_parts = lax.all_to_all(cross_parts, "context", 0, 0, axis_index_groups=lines)
     self_parts = attend(
         self_kernel,
         0,
         queries,
         (span_order,),
-        pl.BlockSpec((key_devices, kv_rows, HEAD_DIM), lambda i: (0, 0, 0)),
-        [pltpu.VMEM((span_keys, HEAD_DIM), BF16)] * 4 + [pltpu.VMEM((1, span_keys), jnp.int32)] * 2,
+        whole(pltpu.HBM),
+        [pltpu.VMEM((key_devices, 2 * rows, HEAD_DIM), BF16)]
+        + [pltpu.VMEM((span_keys, HEAD_DIM), BF16)] * 4
+        + [pltpu.VMEM((1, span_keys), jnp.int32)] * 2
+        + [pltpu.SemaphoreType.DMA((COPIES,))],
     )
-    self_parts = lax.all_to_all(self_parts, "context", 0, 0, axis_index_groups=patches)
+    self_parts = lax.all_to_all(self_parts, "context", 0, 0, axis_index_groups=lines)
     out_shape = jax.ShapeDtypeStruct((rows, heads * HEAD_DIM), BF16)
+    small = pltpu.CompilerParams(vmem_limit_bytes=16 * 1024 * 1024)
     cross_out = pl.pallas_call(
         cross_combine_kernel,
         in_specs=[whole()],
         out_specs=whole(),
         out_shape=out_shape,
+        compiler_params=small,
         name="cross_combine",
     )(cross_parts)
     self_out = pl.pallas_call(
@@ -392,6 +395,7 @@
         in_specs=[whole(pltpu.SMEM), whole()],
         out_specs=whole(),
         out_shape=out_shape,
+        compiler_params=small,
         name="self_combine",
     )(span_order, self_parts)
     return self_out, cross_out

time: 185 us -> 177 us (0.957); the launches traced: 185 us -> 174 us
  waiting for transfers between devices: 114 us -> 85.6 us
  blocking collectives: 15.7 us -> 39.3 us
  starting transfers between devices: 16.2 us -> 10.5 us
    all_gather x1, waiting for transfers between devices: 92.2 us -> 63.8 us  [attention(): keys = lax.all_gather(keys, 'context', axis_index_groups=columns)]
    all_to_all x1 -> x2, blocking collectives: 15.7 us -> 39.3 us  [the longest x1 27.5 us: attention(): queries = lax.all_to_all(queries, 'context', 0, 0, axis_index_groups=lines)]
    all_to_all x3 -> x2, starting transfers between devices: 16.1 us -> 10.5 us  [the longest x1 6.73 us: attention(): lax.all_to_all(cross_parts, 'context', 0, 0, axis_index_groups=lines)]
    all_to_all x3 -> x2, waiting for transfers between devices: 20.8 us -> 21.7 us  [the longest x1 16.6 us: attention(): lax.all_to_all(self_parts, 'context', 0, 0, axis_index_groups=lines)]
  transfers between devices with their start and end apart: 4 -> 3, of which waited for: 3 -> 3; matrix products, arithmetic and copies ran while one was open for 0% -> 0% of each run, Pallas kernels for 7% -> 7%
where the time goes in v4:
time: 177 us; the launch traced here: 174 us
  waiting for transfers between devices  85.6 us (48%)
  blocking collectives  39.3 us (22%)
  Pallas kernels  22 us (12%)
  between operations  14.1 us (8%)
  starting transfers between devices  10.5 us (6%)
  local copies, waits for them, and re-layouts  2.91 us (2%)
    all_gather x1, waiting for transfers between devices, attention(): keys = lax.all_gather(keys, 'context', axis_index_groups=columns)  63.8 us
    all_to_all x1, blocking collectives, attention(): queries = lax.all_to_all(queries, 'context', 0, 0, axis_index_groups=lines)  27.5 us
    all_to_all x1, waiting for transfers between devices, attention(): lax.all_to_all(self_parts, 'context', 0, 0, axis_index_groups=lines)  16.6 us
    pallas_call x2, Pallas kernels, attend(): pl.pallas_call(lambda *refs: kernel(rows, *refs), grid=(RING // STEP,), i...  15.9 us
    all_to_all x1, blocking collectives, attention(): keys = lax.all_to_all(keys, 'context', 0, 0, axis_index_groups=squares)  11.9 us
    all_to_all x1, starting transfers between devices, attention(): lax.all_to_all(cross_parts, 'context', 0, 0, axis_index_groups=lines)  6.73 us
    all_to_all x1, waiting for transfers between devices, attention(): lax.all_to_all(cross_parts, 'context', 0, 0, axis_index_groups=lines)  5.16 us
    all_to_all x1, starting transfers between devices, attention(): lax.all_to_all(self_parts, 'context', 0, 0, axis_index_groups=lines)  3.75 us
  transfers between devices with their start and end apart: 3, of which 3 were waited for; matrix products, arithmetic and copies ran while one was open for 0% of the time, Pallas kernels for 7%

profile of v4, /device:TPU:65, one launch (start us, length us, event | category | flops | bytes accessed | tf_op | source)
XLA Modules:
  0.0 174.5 jit_solution(1948511616508265404)
XLA Ops:
  7.2 0.1 all-gather.3.cloned.1.call-start
  7.2 2.6 %prepare.1 = (bf16[8,640,128]{2,1,0:T(8,128)(2,1)}, bf16[4,208,128]{2,1,0:T(8,128)(2,1)}) custom-call(s32[256]{0:T(256)} %order.3, f32[1,128]{1,0:T(1,128)} %constant.2.clone.freq, bf16[80,1024]{1,0:T(8,128)(2,1)} %sq.1, bf16[80,256]{1,0:T(8,128)(2,1)} %sk.1, bf16[80,256]{1,0:T(8,128)(2,1)} %sv.1, bf16[80,1024]{1,0:T(8,128)(2,1)} %cq.1, bf16[24,256]{1,0:T(8,128)(2,1)} %ck.1, ...), custom_call_target="tpu_custom_call" | custom-call | tf_op jit(solution)/shard_map/prepare/pallas_call | solution.py:310
  9.8 11.9 %all_to_all.20 = bf16[4,208,128]{2,1,0:T(8,128)(2,1)} all-to-all(bf16[4,208,128]{2,1,0:T(8,128)(2,1)} %get-tuple-element.5), channel_id=1, replica_groups={{0,2,16,18},{4,6,20,22},{8,10,24,26},{12,14,28,30},{32,34,48,50},{36,38..., dimensions={0} | all-to-all | bytes 425984 | tf_op jit(solution)/shard_map/all_to_all | solution.py:329
  21.7 0.1 all-gather.3.cloned.1.call-update
  21.7 27.5 %all_to_all.21.refs_1_.refs_0_ = bf16[8,640,128]{2,1,0:T(8,128)(2,1)S(1)} all-to-all(bf16[8,640,128]{2,1,0:T(8,128)(2,1)} %get-tuple-element.4), channel_id=1, replica_groups={{0,2,4,6,8,10,12,14},{16,18,20,22,24,26,28,30},{32,34,36,38,40,42,44,46..., dimensions={0} | all-to-all | bytes 2621440 | tf_op jit(solution)/shard_map/all_to_all | solution.py:331
  49.2 63.8 %all-gather.3.cloned.1.call-done.refs_2_.refs_1_ = bf16[32,208,128]{2,1,0:T(8,128)(2,1)} async-done(((bf16[4,208,128]{2,1,0:T(8,128)(2,1)}), bf16[32,208,128]{2,1,0:T(8,128)(2,1)}) %all-gather.3.cloned.1.call-update) | async-done | bytes 1703952 | tf_op jit(solution)/shard_map/all_gather | solution.py:330
  113.0 0.0 copy-start.1
  113.0 1.5 copy-done.1
  114.5 4.5 %shard_map.96 = bf16[8,328,128]{2,1,0:T(8,128)(2,1)} custom-call(bf16[8,640,128]{2,1,0:T(8,128)(2,1)S(1)} %all_to_all.21.refs_1_.refs_0_, bf16[32,208,128]{2,1,0:T(8,128)(2,1)S(1)} %copy-done.1), custom_call_target="tpu_custom_call" | custom-call | flops 3355443200 | bytes 1703936 | tf_op jit(solution)/shard_map/pallas_call | solution.py:337
  119.0 0.0 copy-start
  119.0 6.7 %all-to-all-start.3 = ((bf16[8,328,128]{2,1,0:T(8,128)(2,1)}), bf16[8,328,128]{2,1,0:T(8,128)(2,1)S(1)}, u32[]{:S(2)}, u32[]{:S(2)}) async-start(bf16[8,328,128]{2,1,0:T(8,128)(2,1)} %shard_map.96), calls=%async_computation.3 | async-start | bytes 1343488 | tf_op jit(solution)/shard_map/all_to_all | solution.py:370
  125.7 0.0 copy-done
  125.7 0.0 copy-start.2
  125.7 1.4 copy-done.2
  127.2 11.4 %shard_map.95 = bf16[8,328,128]{2,1,0:T(8,128)(2,1)} custom-call(s32[256]{0:T(256)S(1)} %copy-done, bf16[8,640,128]{2,1,0:T(8,128)(2,1)S(1)} %all_to_all.21.refs_1_.refs_0_, bf16[32,208,128]{2,1,0:T(8,128)(2,1)S(1)} %copy-done.2), custom_call_target="tpu_custom_call" | custom-call | flops 3355443200 | bytes 1703936 | tf_op jit(solution)/shard_map/pallas_call | solution.py:337
  138.6 5.2 %all-to-all-done.3.parts = bf16[8,328,128]{2,1,0:T(8,128)(2,1)S(1)} async-done(((bf16[8,328,128]{2,1,0:T(8,128)(2,1)}), bf16[8,328,128]{2,1,0:T(8,128)(2,1)S(1)}, u32[]{:S(2)}, u32[]{:S(2)}) %all-to-all-start.3) | async-done | bytes 671776 | tf_op jit(solution)/shard_map/all_to_all | solution.py:370
  143.8 3.7 %all-to-all-start.2 = ((bf16[8,328,128]{2,1,0:T(8,128)(2,1)}), bf16[8,328,128]{2,1,0:T(8,128)(2,1)S(1)}, u32[]{:S(2)}, u32[]{:S(2)}) async-start(bf16[8,328,128]{2,1,0:T(8,128)(2,1)} %shard_map.95), calls=%async_computation.2 | async-start | bytes 1343488 | tf_op jit(solution)/shard_map/all_to_all | solution.py:382
  147.5 1.5 cross_combine.1
  149.0 16.6 %all-to-all-done.2.parts = bf16[8,328,128]{2,1,0:T(8,128)(2,1)S(1)} async-done(((bf16[8,328,128]{2,1,0:T(8,128)(2,1)}), bf16[8,328,128]{2,1,0:T(8,128)(2,1)S(1)}, u32[]{:S(2)}, u32[]{:S(2)}) %all-to-all-start.2) | async-done | bytes 671776 | tf_op jit(solution)/shard_map/all_to_all | solution.py:382
  165.6 2.0 %self_combine.1 = bf16[80,1024]{1,0:T(8,128)(2,1)} custom-call(s32[256]{0:T(256)S(1)} %copy-done, bf16[8,328,128]{2,1,0:T(8,128)(2,1)S(1)} %all-to-all-done.2.parts), custom_call_target="tpu_custom_call" | custom-call | tf_op jit(solution)/shard_map/self_combine/pallas_call | solution.py:393
Async XLA Ops:
  7.2 105.8 %all-gather.3.cloned.1.call-start = ((), (), s32[]{:S(2)}) async-start(), calls=%async_computation.4 | async-start | bytes 1916928 | tf_op jit(solution)/shard_map/all_gather | solution.py:330
  113.0 1.5 copy-start.1
  119.0 6.7 %copy-start = (s32[256]{0:T(256)S(1)}, s32[256]{0:T(256)}, u32[]{:S(2)}) copy-start(s32[256]{0:T(256)} %order.3) | copy-start | bytes 3076
  119.0 24.8 %all-to-all-start.3 = ((bf16[8,328,128]{2,1,0:T(8,128)(2,1)}), bf16[8,328,128]{2,1,0:T(8,128)(2,1)S(1)}, u32[]{:S(2)}, u32[]{:S(2)}) async-start(bf16[8,328,128]{2,1,0:T(8,128)(2,1)} %shard_map.96), calls=%async_computation.3 | async-start | bytes 1343488 | tf_op jit(solution)/shard_map/all_to_all | solution.py:370
  125.7 1.5 copy-start.2
  143.8 21.8 %all-to-all-start.2 = ((bf16[8,328,128]{2,1,0:T(8,128)(2,1)}), bf16[8,328,128]{2,1,0:T(8,128)(2,1)S(1)}, u32[]{:S(2)}, u32[]{:S(2)}) async-start(bf16[8,328,128]{2,1,0:T(8,128)(2,1)} %shard_map.95), calls=%async_computation.2 | async-start | bytes 1343488 | tf_op jit(solution)/shard_map/all_to_all | solution.py:382
Sparse Core Ops, SparseCore 0:
  21.9 91.1 all-gather.2

commit v5 on v4

--- a/solution.py
+++ b/solution.py
@@ -13,7 +13,6 @@
 GROUP = HEADS // KV_HEADS
 RING = 8
 PAIR = 2
-COPIES = 8
 STEP = 4
 LEVEL_ROWS = 8
 NEG_FILL = -1e30
@@ -141,18 +140,7 @@
     return whole_rows + [rows[6:7] + pltpu.roll(rows[6:7], HEAD_DIM // 2, 1) + rows[7:8]]
 
 
-def gathered_rows(kv_hbm, low, kv_in, sems, targets):
-    chunk = kv_in.shape[0] // sems.shape[0]
-    rows = pl.ds(low, kv_in.shape[1])
-    copies = [
-        pltpu.make_async_copy(
-            kv_hbm.at[pl.ds(c * chunk, chunk), rows, :], kv_in.at[pl.ds(c * chunk, chunk)], sems.at[c]
-        )
-        for c in range(sems.shape[0])
-    ]
-    for copy in copies:
-        copy.start()
-
+def sort_rows(kv_in, first, last, targets):
     def pair(i, carry):
         a = kv_in[2 * i].astype(F32)
         b = kv_in[2 * i + 1].astype(F32)
@@ -162,39 +150,48 @@
             ref[pl.ds(at, size), :] = rows_of(a[lo:hi], b[lo:hi]).astype(BF16)
         return carry
 
-    for c, copy in enumerate(copies):
-        copy.wait()
-        lax.fori_loop(c * chunk // 2, (c + 1) * chunk // 2, pair, 0)
-
-
-def cross_kernel(rows, q_in, kv_hbm, out, kv_in, key, val, sems):
-    image = kv_in.shape[1] // 2
+    lax.fori_loop(first // 2, last // 2, pair, 0)
+
+
+def cross_kernel(rows, q_in, kv_in, out, key, val):
+    devices, image = kv_in.shape[0], kv_in.shape[1] // 2
 
     @pl.when(pl.program_id(0) == 0)
     def _():
-        targets = [(key, 0, image), (val, image, 2 * image)]
-        gathered_rows(kv_hbm, 2 * rows, kv_in, sems, targets)
+        sort_rows(kv_in, 0, devices, [(key, 0, image), (val, image, 2 * image)])
 
     s = [scores(q_in[i], key) for i in range(STEP)]
     for i in range(STEP):
         out[i] = with_levels(*finish([(s[i], val)]))
 
 
+def places_kernel(span, devices, order, pos_e, pos_l):
+    low = lax.axis_index("context") % RING // PAIR * PAIR
+    lane = lax.broadcasted_iota(jnp.int32, pos_e.shape, 1)
+    place_e, place_l = lane, lane
+    for d in range(devices):
+        early, late = spans_of(order, d // PAIR * RING + low + d % PAIR)
+        here = lane >= d * span
+        place_e = jnp.where(here, lane + (early - d) * span, place_e)
+        place_l = jnp.where(here, lane + (late - d) * span, place_l)
+    pos_e[...] = place_e
+    pos_l[...] = place_l
+
+
 def self_kernel(
-    rows, order, q_in, kv_hbm, out, kv_in, key_e, key_l, val_e, val_l, pos_e, pos_l, sems
+    rows, order, q_in, kv_in, pos_e, pos_l, out, key_e, key_l, val_e, val_l
 ):
     step = pl.program_id(0)
     me = lax.axis_index("context")
-    line, column = me // RING, me % RING
+    line = me // RING
     span = rows // 2
 
     @pl.when(step == 0)
     def _():
-        gathered_rows(
-            kv_hbm,
+        sort_rows(
+            kv_in,
             0,
-            kv_in,
-            sems,
+            kv_in.shape[0],
             [
                 (key_e, 0, span),
                 (key_l, span, rows),
@@ -202,16 +199,6 @@
                 (val_l, rows + span, 2 * rows),
             ],
         )
-        low = column // PAIR * PAIR
-        lane = lax.broadcasted_iota(jnp.int32, pos_e.shape, 1)
-        place_e, place_l = lane, lane
-        for d in range(kv_in.shape[0]):
-            early, late = spans_of(order, d // PAIR * RING + low + d % PAIR)
-            here = lane >= d * span
-            place_e = jnp.where(here, lane + (early - d) * span, place_e)
-            place_l = jnp.where(here, lane + (late - d) * span, place_l)
-        pos_e[...] = place_e
-        pos_l[...] = place_l
 
     size = GROUP * span
     within = lax.broadcasted_iota(jnp.int32, (size, 1), 0) % span
@@ -327,21 +314,43 @@
         cross_values,
     )
     keys = lax.all_to_all(keys, "context", 0, 0, axis_index_groups=squares)
-    keys = lax.all_gather(keys, "context", axis_index_groups=columns)
+    text, picture = keys[:, : 2 * rows, :], keys[:, 2 * rows :, :]
+    text = lax.all_gather(text, "context", axis_index_groups=columns)
+    far = height // PAIR // 2
+    while far:
+        ring = [
+            (z * RING + x, (z + far * PAIR) % height * RING + x)
+            for z in range(height)
+            for x in range(RING)
+        ]
+        more = lax.ppermute(picture, "context", ring)
+        picture = jnp.concatenate([picture, more], 0)
+        far = far // 2
     queries = lax.all_to_all(queries, "context", 0, 0, axis_index_groups=lines)
-    keys = keys.reshape(key_devices, kv_rows, HEAD_DIM)
-
+    text = text.reshape(key_devices, 2 * rows, HEAD_DIM)
+    picture = picture.reshape(key_devices, 2 * image, HEAD_DIM)
+
+    span_keys = key_devices * rows // 2
+    image_keys = key_devices * image
+    places = pl.pallas_call(
+        lambda *refs: places_kernel(rows // 2, key_devices, *refs),
+        in_specs=[whole(pltpu.SMEM)],
+        out_specs=[whole(), whole()],
+        out_shape=[jax.ShapeDtypeStruct((1, span_keys), jnp.int32)] * 2,
+        name="places",
+    )(span_order)
     out_rows = size + LEVEL_ROWS
 
-    def attend(kernel, half, queries, order, kv_spec, scratch):
+    def attend(kernel, half, keys, order, places, scratch):
         return pl.pallas_call(
             lambda *refs: kernel(rows, *refs),
             grid=(RING // STEP,),
             in_specs=[whole(pltpu.SMEM)] * len(order)
             + [
                 pl.BlockSpec((STEP, size, HEAD_DIM), lambda i: (i, half, 0)),
-                kv_spec,
-            ],
+                pl.BlockSpec(keys.shape, lambda i: (0, 0, 0)),
+            ]
+            + [pl.BlockSpec(p.shape, lambda i: (0, 0)) for p in places],
             out_specs=pl.BlockSpec((STEP, out_rows, HEAD_DIM), lambda i: (i, 0, 0)),
             out_shape=jax.ShapeDtypeStruct((RING, out_rows, HEAD_DIM), BF16),
             scratch_shapes=scratch,
@@ -353,31 +362,14 @@
                 transcendentals=RING * size * key_devices * rows,
                 bytes_accessed=2 * key_devices * kv_rows * HEAD_DIM,
             ),
-        )(*order, queries, keys)
-
-    span_keys = key_devices * rows // 2
-    image_keys = key_devices * image
+        )(*order, queries, keys, *places)
+
     cross_parts = attend(
-        cross_kernel,
-        1,
-        queries,
-        (),
-        whole(pltpu.HBM),
-        [pltpu.VMEM((key_devices, 2 * image, HEAD_DIM), BF16)]
-        + [pltpu.VMEM((image_keys, HEAD_DIM), BF16)] * 2
-        + [pltpu.SemaphoreType.DMA((COPIES,))],
+        cross_kernel, 1, picture, (), (), [pltpu.VMEM((image_keys, HEAD_DIM), BF16)] * 2
     )
     cross_parts = lax.all_to_all(cross_parts, "context", 0, 0, axis_index_groups=lines)
     self_parts = attend(
-        self_kernel,
-        0,
-        queries,
-        (span_order,),
-        whole(pltpu.HBM),
-        [pltpu.VMEM((key_devices, 2 * rows, HEAD_DIM), BF16)]
-        + [pltpu.VMEM((span_keys, HEAD_DIM), BF16)] * 4
-        + [pltpu.VMEM((1, span_keys), jnp.int32)] * 2
-        + [pltpu.SemaphoreType.DMA((COPIES,))],
+        self_kernel, 0, text, (span_order,), places, [pltpu.VMEM((span_keys, HEAD_DIM), BF16)] * 4
     )
     self_parts = lax.all_to_all(self_parts, "context", 0, 0, axis_index_groups=lines)
     out_shape = jax.ShapeDtypeStruct((rows, heads * HEAD_DIM), BF16)

time: 177 us -> 185 us (1.045)
  starting transfers between devices: 10.5 us -> 70 us
  blocking collectives: 39.3 us -> 11.4 us
  waiting for transfers between devices: 85.6 us -> 63.2 us
    all_gather x1, waiting for transfers between devices: 63.8 us -> 0.01 us  [attention(): text = lax.all_gather(text, 'context', axis_index_groups=columns)]
    ppermute x0 -> x3, starting transfers between devices: none -> 53.9 us  [attention(): more = lax.ppermute(picture, 'context', ring)]
    ppermute x0 -> x3, waiting for transfers between devices: none -> 38.6 us  [attention(): more = lax.ppermute(picture, 'context', ring)]
    all_to_all x1 -> x0, blocking collectives: 27.5 us -> none  [attention(): queries = lax.all_to_all(queries, 'context', 0, 0, axis_index_groups=lines)]
    all_to_all x0 -> x1, starting transfers between devices: none -> 6.53 us  [attention(): queries = lax.all_to_all(queries, 'context', 0, 0, axis_index_groups=lines)]
  transfers between devices with their start and end apart: 3 -> 7, of which waited for: 3 -> 5; matrix products, arithmetic and copies ran while one was open for 0% -> 0% of each run, Pallas kernels for 7% -> 9%
where the time goes in v5:
time: 185 us; the launch traced here: 184 us
  starting transfers between devices  70 us (38%)
  waiting for transfers between devices  63.2 us (34%)
  Pallas kernels  21.9 us (12%)
  between operations  14.1 us (8%)
  blocking collectives  11.4 us (6%)
  local copies, waits for them, and re-layouts  3.38 us (2%)
    ppermute x3, starting transfers between devices, attention(): more = lax.ppermute(picture, 'context', ring)  53.9 us
    ppermute x3, waiting for transfers between devices, attention(): more = lax.ppermute(picture, 'context', ring)  38.6 us
    all_to_all x1, waiting for transfers between devices, attention(): lax.all_to_all(self_parts, 'context', 0, 0, axis_index_groups=lines)  17.7 us
    pallas_call x2, Pallas kernels, attend(): pl.pallas_call(lambda *refs: kernel(rows, *refs), grid=(RING // STEP,), i...  14.4 us
    all_to_all x1, blocking collectives, attention(): keys = lax.all_to_all(keys, 'context', 0, 0, axis_index_groups=squares)  11.4 us
    all_to_all x1, waiting for transfers between devices, attention(): lax.all_to_all(cross_parts, 'context', 0, 0, axis_index_groups=lines)  6.85 us
    all_to_all x1, starting transfers between devices, attention(): queries = lax.all_to_all(queries, 'context', 0, 0, axis_index_groups=lines)  6.53 us
    all_to_all x1, starting transfers between devices, attention(): lax.all_to_all(cross_parts, 'context', 0, 0, axis_index_groups=lines)  5.81 us
  transfers between devices with their start and end apart: 7, of which 5 were waited for; matrix products, arithmetic and copies ran while one was open for 0% of the time, Pallas kernels for 9%

profile of v5, /device:TPU:65, one launch (start us, length us, event | category | flops | bytes accessed | tf_op | source)
XLA Modules:
  0.0 184.1 jit_solution(13684323268096538082)
XLA Ops:
  7.2 2.5 %prepare.1 = (bf16[8,640,128]{2,1,0:T(8,128)(2,1)}, bf16[4,208,128]{2,1,0:T(8,128)(2,1)}) custom-call(s32[256]{0:T(256)} %order.3, f32[1,128]{1,0:T(1,128)} %constant.2.clone.freq, bf16[80,1024]{1,0:T(8,128)(2,1)} %sq.1, bf16[80,256]{1,0:T(8,128)(2,1)} %sk.1, bf16[80,256]{1,0:T(8,128)(2,1)} %sv.1, bf16[80,1024]{1,0:T(8,128)(2,1)} %cq.1, bf16[24,256]{1,0:T(8,128)(2,1)} %ck.1, ...), custom_call_target="tpu_custom_call" | custom-call | tf_op jit(solution)/shard_map/prepare/pallas_call | solution.py:297
  9.7 11.4 %all_to_all.20 = bf16[4,208,128]{2,1,0:T(8,128)(2,1)S(1)} all-to-all(bf16[4,208,128]{2,1,0:T(8,128)(2,1)} %get-tuple-element.7), channel_id=1, replica_groups={{0,2,16,18},{4,6,20,22},{8,10,24,26},{12,14,28,30},{32,34,48,50},{36,38..., dimensions={0} | all-to-all | bytes 425984 | tf_op jit(solution)/shard_map/all_to_all | solution.py:316
  21.1 6.5 %all-to-all-start = ((bf16[8,640,128]{2,1,0:T(8,128)(2,1)}), bf16[8,640,128]{2,1,0:T(8,128)(2,1)S(1)}, u32[]{:S(2)}, u32[]{:S(2)}) async-start(bf16[8,640,128]{2,1,0:T(8,128)(2,1)} %get-tuple-element.6), calls=%async_computation | async-start | bytes 2621440 | tf_op jit(solution)/shard_map/all_to_all | solution.py:329
  27.7 0.1 all-gather.3.cloned.1.call-start
  27.7 0.7 slice.8
  28.4 0.1 all-gather.3.cloned.1.call-update
  28.5 32.0 %collective-permute-start = (bf16[4,48,128]{2,1,0:T(8,128)(2,1)S(1)}, bf16[4,48,128]{2,1,0:T(8,128)(2,1)S(1)}, u32[]{:S(2)}, u32[]{:S(2)}) collective-permute-start(bf16[4,48,128]{2,1,0:T(8,128)(2,1)S(1)} %slice.9), channel_id=1, source_target_pairs={{0,128},{2,130},{4,132},{6,134},{8,136},{10,138},{12,140},{14,142}... | collective-permute-start | bytes 147464 | tf_op jit(solution)/shard_map/ppermute | solution.py:326
  60.4 1.5 collective-permute-done
  61.9 13.2 %collective-permute-start.1 = (bf16[8,48,128]{2,1,0:T(8,128)(2,1)S(1)}, bf16[8,48,128]{2,1,0:T(8,128)(2,1)S(1)}, u32[]{:S(2)}, u32[]{:S(2)}) collective-permute-start(bf16[8,48,128]{2,1,0:T(8,128)(2,1)S(1)} %pad_maximum_fusion.2), channel_id=1, source_target_pairs={{0,64},{2,66},{4,68},{6,70},{8,72},{10,74},{12,76},{14,78},{16,80}... | collective-permute-start | bytes 294920 | tf_op jit(solution)/shard_map/ppermute | solution.py:326
  75.2 7.0 %collective-permute-done.1 = bf16[8,48,128]{2,1,0:T(8,128)(2,1)S(1)} collective-permute-done((bf16[8,48,128]{2,1,0:T(8,128)(2,1)S(1)}, bf16[8,48,128]{2,1,0:T(8,128)(2,1)S(1)}, u32[]{:S(2)}, u32[]{:S(2)}) %collective-permute-start.1) | collective-permute-done | bytes 98336 | tf_op jit(solution)/shard_map/ppermute | solution.py:326
  82.2 8.7 %collective-permute-start.2 = (bf16[16,48,128]{2,1,0:T(8,128)(2,1)S(1)}, bf16[16,48,128]{2,1,0:T(8,128)(2,1)S(1)}, u32[]{:S(2)}, u32[]{:S(2)}) collective-permute-start(bf16[16,48,128]{2,1,0:T(8,128)(2,1)S(1)} %pad_maximum_fusion.1), channel_id=1, source_target_pairs={{0,32},{2,34},{4,36},{6,38},{8,40},{10,42},{12,44},{14,46},{16,48}... | collective-permute-start | bytes 589832 | tf_op jit(solution)/shard_map/ppermute | solution.py:326
  90.9 30.1 %collective-permute-done.2 = bf16[16,48,128]{2,1,0:T(8,128)(2,1)S(1)} collective-permute-done((bf16[16,48,128]{2,1,0:T(8,128)(2,1)S(1)}, bf16[16,48,128]{2,1,0:T(8,128)(2,1)S(1)}, u32[]{:S(2)}, u32[]{:S(2)}) %collective-permute-start.2) | collective-permute-done | bytes 196640 | tf_op jit(solution)/shard_map/ppermute | solution.py:326
  121.1 0.0 all-to-all-done.refs_1_.refs_0_
  121.1 4.3 %shard_map.96 = bf16[8,328,128]{2,1,0:T(8,128)(2,1)} custom-call(bf16[8,640,128]{2,1,0:T(8,128)(2,1)S(1)} %all-to-all-done.refs_1_.refs_0_, bf16[32,48,128]{2,1,0:T(8,128)(2,1)S(1)} %pad_maximum_fusion.refs_1_), custom_call_target="tpu_custom_call" | custom-call | flops 3355443200 | bytes 1703936 | tf_op jit(solution)/shard_map/pallas_call | solution.py:345
  125.4 0.0 copy-start
  125.4 5.8 %all-to-all-start.3 = ((bf16[8,328,128]{2,1,0:T(8,128)(2,1)}), bf16[8,328,128]{2,1,0:T(8,128)(2,1)S(1)}, u32[]{:S(2)}, u32[]{:S(2)}) async-start(bf16[8,328,128]{2,1,0:T(8,128)(2,1)} %shard_map.96), calls=%async_computation.3 | async-start | bytes 1343488 | tf_op jit(solution)/shard_map/all_to_all | solution.py:370
  131.2 1.5 places.1
  132.7 0.0 all-gather.3.cloned.1.call-done.refs_2_
  132.7 0.0 copy-done
  132.7 0.0 copy-start.1
  132.7 1.3 copy-done.1
  134.0 0.0 copy-start.2
  134.0 0.7 copy-done.2
  134.7 0.0 copy-start.3
  134.7 0.7 copy-done.3
  135.4 10.1 %shard_map.95 = bf16[8,328,128]{2,1,0:T(8,128)(2,1)} custom-call(s32[256]{0:T(256)S(1)} %copy-done, bf16[8,640,128]{2,1,0:T(8,128)(2,1)S(1)} %all-to-all-done.refs_1_.refs_0_, bf16[32,160,128]{2,1,0:T(8,128)(2,1)S(1)} %copy-done.1, s32[1,1280]{1,0:T(1,128)S(1)} %copy-done.2, s32[1,1280]{1,0:T(1,128)S(1)} %copy-done.3), custom_call_target="tpu_custom_call" | custom-call | flops 3355443200 | bytes 1703936 | tf_op jit(solution)/shard_map/pallas_call | solution.py:345
  145.5 6.9 %all-to-all-done.3.parts = bf16[8,328,128]{2,1,0:T(8,128)(2,1)S(1)} async-done(((bf16[8,328,128]{2,1,0:T(8,128)(2,1)}), bf16[8,328,128]{2,1,0:T(8,128)(2,1)S(1)}, u32[]{:S(2)}, u32[]{:S(2)}) %all-to-all-start.3) | async-done | bytes 671776 | tf_op jit(solution)/shard_map/all_to_all | solution.py:370
  152.4 3.7 %all-to-all-start.2 = ((bf16[8,328,128]{2,1,0:T(8,128)(2,1)}), bf16[8,328,128]{2,1,0:T(8,128)(2,1)S(1)}, u32[]{:S(2)}, u32[]{:S(2)}) async-start(bf16[8,328,128]{2,1,0:T(8,128)(2,1)} %shard_map.95), calls=%async_computation.2 | async-start | bytes 1343488 | tf_op jit(solution)/shard_map/all_to_all | solution.py:374
  156.1 1.5 cross_combine.1
  157.6 17.7 %all-to-all-done.2.parts = bf16[8,328,128]{2,1,0:T(8,128)(2,1)S(1)} async-done(((bf16[8,328,128]{2,1,0:T(8,128)(2,1)}), bf16[8,328,128]{2,1,0:T(8,128)(2,1)S(1)}, u32[]{:S(2)}, u32[]{:S(2)}) %all-to-all-start.2) | async-done | bytes 671776 | tf_op jit(solution)/shard_map/all_to_all | solution.py:374
  175.3 2.0 %self_combine.1 = bf16[80,1024]{1,0:T(8,128)(2,1)} custom-call(s32[256]{0:T(256)S(1)} %copy-done, bf16[8,328,128]{2,1,0:T(8,128)(2,1)S(1)} %all-to-all-done.2.parts), custom_call_target="tpu_custom_call" | custom-call | tf_op jit(solution)/shard_map/self_combine/pallas_call | solution.py:385
  (4 shorter events, 0.1 us)
Async XLA Ops:
  21.1 100.0 %all-to-all-start = ((bf16[8,640,128]{2,1,0:T(8,128)(2,1)}), bf16[8,640,128]{2,1,0:T(8,128)(2,1)S(1)}, u32[]{:S(2)}, u32[]{:S(2)}) async-start(bf16[8,640,128]{2,1,0:T(8,128)(2,1)} %get-tuple-element.6), calls=%async_computation | async-start | bytes 2621440 | tf_op jit(solution)/shard_map/all_to_all | solution.py:329
  27.7 105.0 %all-gather.3.cloned.1.call-start = ((), (), s32[]{:S(2)}) async-start(), calls=%async_computation.4 | async-start | bytes 1474560 | tf_op jit(solution)/shard_map/all_gather | solution.py:318
  28.5 33.4 %collective-permute-start = (bf16[4,48,128]{2,1,0:T(8,128)(2,1)S(1)}, bf16[4,48,128]{2,1,0:T(8,128)(2,1)S(1)}, u32[]{:S(2)}, u32[]{:S(2)}) collective-permute-start(bf16[4,48,128]{2,1,0:T(8,128)(2,1)S(1)} %slice.9), channel_id=1, source_target_pairs={{0,128},{2,130},{4,132},{6,134},{8,136},{10,138},{12,140},{14,142}... | collective-permute-start | bytes 147464 | tf_op jit(solution)/shard_map/ppermute | solution.py:326
  61.9 20.3 %collective-permute-start.1 = (bf16[8,48,128]{2,1,0:T(8,128)(2,1)S(1)}, bf16[8,48,128]{2,1,0:T(8,128)(2,1)S(1)}, u32[]{:S(2)}, u32[]{:S(2)}) collective-permute-start(bf16[8,48,128]{2,1,0:T(8,128)(2,1)S(1)} %pad_maximum_fusion.2), channel_id=1, source_target_pairs={{0,64},{2,66},{4,68},{6,70},{8,72},{10,74},{12,76},{14,78},{16,80}... | collective-permute-start | bytes 294920 | tf_op jit(solution)/shard_map/ppermute | solution.py:326
  82.2 38.9 %collective-permute-start.2 = (bf16[16,48,128]{2,1,0:T(8,128)(2,1)S(1)}, bf16[16,48,128]{2,1,0:T(8,128)(2,1)S(1)}, u32[]{:S(2)}, u32[]{:S(2)}) collective-permute-start(bf16[16,48,128]{2,1,0:T(8,128)(2,1)S(1)} %pad_maximum_fusion.1), channel_id=1, source_target_pairs={{0,32},{2,34},{4,36},{6,38},{8,40},{10,42},{12,44},{14,46},{16,48}... | collective-permute-start | bytes 589832 | tf_op jit(solution)/shard_map/ppermute | solution.py:326
  125.4 7.3 %copy-start = (s32[256]{0:T(256)S(1)}, s32[256]{0:T(256)}, u32[]{:S(2)}) copy-start(s32[256]{0:T(256)} %order.3) | copy-start | bytes 3076
  125.4 26.9 %all-to-all-start.3 = ((bf16[8,328,128]{2,1,0:T(8,128)(2,1)}), bf16[8,328,128]{2,1,0:T(8,128)(2,1)S(1)}, u32[]{:S(2)}, u32[]{:S(2)}) async-start(bf16[8,328,128]{2,1,0:T(8,128)(2,1)} %shard_map.96), calls=%async_computation.3 | async-start | bytes 1343488 | tf_op jit(solution)/shard_map/all_to_all | solution.py:370
  132.7 1.3 copy-start.1
  134.0 0.7 copy-start.2
  134.7 0.7 copy-start.3
  152.4 22.9 %all-to-all-start.2 = ((bf16[8,328,128]{2,1,0:T(8,128)(2,1)}), bf16[8,328,128]{2,1,0:T(8,128)(2,1)S(1)}, u32[]{:S(2)}, u32[]{:S(2)}) async-start(bf16[8,328,128]{2,1,0:T(8,128)(2,1)} %shard_map.95), calls=%async_computation.2 | async-start | bytes 1343488 | tf_op jit(solution)/shard_map/all_to_all | solution.py:374
Sparse Core Ops, SparseCore 0:
  31.2 98.4 all-gather.2

commit v6 on v5

--- a/solution.py
+++ b/solution.py
@@ -153,12 +153,15 @@
     lax.fori_loop(first // 2, last // 2, pair, 0)
 
 
-def cross_kernel(rows, q_in, kv_in, out, key, val):
-    devices, image = kv_in.shape[0], kv_in.shape[1] // 2
+def cross_kernel(value_slots, rows, q_in, key_in, val_in, out, key, val):
+    devices, image = key_in.shape[:2]
 
     @pl.when(pl.program_id(0) == 0)
     def _():
-        sort_rows(kv_in, 0, devices, [(key, 0, image), (val, image, 2 * image)])
+        sort_rows(key_in, 0, devices, [(key, 0, image)])
+        for d in range(0, devices, 2):
+            pair = [val_in[value_slots[i]].astype(F32) for i in (d, d + 1)]
+            val[d * image : (d + 2) * image, :] = rows_of(*pair).astype(BF16)
 
     s = [scores(q_in[i], key) for i in range(STEP)]
     for i in range(STEP):
@@ -316,19 +319,25 @@
     keys = lax.all_to_all(keys, "context", 0, 0, axis_index_groups=squares)
     text, picture = keys[:, : 2 * rows, :], keys[:, 2 * rows :, :]
     text = lax.all_gather(text, "context", axis_index_groups=columns)
-    far = height // PAIR // 2
+    turns = height // PAIR
+
+    far = turns // 2
+    picture = jnp.concatenate([picture, shifted(picture, far, height)], 0)
+    picture_keys, picture_values = picture[:, :image, :], picture[:, image:, :]
+    key_order = value_order = [0, -far % turns]
+    far //= 2
     while far:
-        ring = [
-            (z * RING + x, (z + far * PAIR) % height * RING + x)
-            for z in range(height)
-            for x in range(RING)
-        ]
-        more = lax.ppermute(picture, "context", ring)
-        picture = jnp.concatenate([picture, more], 0)
-        far = far // 2
+        more_keys = shifted(picture_keys, far, height)
+        more_values = shifted(picture_values, -far, height)
+        picture_keys = jnp.concatenate([picture_keys, more_keys], 0)
+        picture_values = jnp.concatenate([picture_values, more_values], 0)
+        key_order = key_order + [(o - far) % turns for o in key_order]
+        value_order = value_order + [(o + far) % turns for o in value_order]
+        far //= 2
+    each = PAIR * PAIR
+    value_slots = [value_order.index(o) * each + i for o in key_order for i in range(each)]
     queries = lax.all_to_all(queries, "context", 0, 0, axis_index_groups=lines)
     text = text.reshape(key_devices, 2 * rows, HEAD_DIM)
-    picture = picture.reshape(key_devices, 2 * image, HEAD_DIM)
 
     span_keys = key_devices * rows // 2
     image_keys = key_devices * image
@@ -341,15 +350,15 @@
     )(span_order)
     out_rows = size + LEVEL_ROWS
 
-    def attend(kernel, half, keys, order, places, scratch):
+    def attend(kernel, half, order, keys, places, scratch):
         return pl.pallas_call(
             lambda *refs: kernel(rows, *refs),
             grid=(RING // STEP,),
             in_specs=[whole(pltpu.SMEM)] * len(order)
             + [
                 pl.BlockSpec((STEP, size, HEAD_DIM), lambda i: (i, half, 0)),
-                pl.BlockSpec(keys.shape, lambda i: (0, 0, 0)),
             ]
+            + [pl.BlockSpec(k.shape, lambda i: (0, 0, 0)) for k in keys]
             + [pl.BlockSpec(p.shape, lambda i: (0, 0)) for p in places],
             out_specs=pl.BlockSpec((STEP, out_rows, HEAD_DIM), lambda i: (i, 0, 0)),
             out_shape=jax.ShapeDtypeStruct((RING, out_rows, HEAD_DIM), BF16),
@@ -362,14 +371,24 @@
                 transcendentals=RING * size * key_devices * rows,
                 bytes_accessed=2 * key_devices * kv_rows * HEAD_DIM,
             ),
-        )(*order, queries, keys, *places)
+        )(*order, queries, *keys, *places)
 
     cross_parts = attend(
-        cross_kernel, 1, picture, (), (), [pltpu.VMEM((image_keys, HEAD_DIM), BF16)] * 2
+        lambda *refs: cross_kernel(value_slots, *refs),
+        1,
+        (),
+        (picture_keys, picture_values),
+        (),
+        [pltpu.VMEM((image_keys, HEAD_DIM), BF16)] * 2,
     )
     cross_parts = lax.all_to_all(cross_parts, "context", 0, 0, axis_index_groups=lines)
     self_parts = attend(
-        self_kernel, 0, text, (span_order,), places, [pltpu.VMEM((span_keys, HEAD_DIM), BF16)] * 4
+        self_kernel,
+        0,
+        (span_order,),
+        (text,),
+        places,
+        [pltpu.VMEM((span_keys, HEAD_DIM), BF16)] * 4,
     )
     self_parts = lax.all_to_all(self_parts, "context", 0, 0, axis_index_groups=lines)
     out_shape = jax.ShapeDtypeStruct((rows, heads * HEAD_DIM), BF16)
@@ -393,6 +412,15 @@
     return self_out, cross_out
 
 
+def shifted(x, far, height):
+    ring = [
+        (z * RING + c, (z + far * PAIR) % height * RING + c)
+        for z in range(height)
+        for c in range(RING)
+    ]
+    return lax.ppermute(x, "context", ring)
+
+
 def solution(mesh):
     rows = P(("groups", "context"), "tensor")
     return jax.shard_map(

time: 185 us -> 171 us (0.924)
  waiting for transfers between devices: 63.2 us -> 27 us
  starting transfers between devices: 70 us -> 91.2 us
    ppermute x3 -> x5, waiting for transfers between devices: 38.6 us -> 7.28 us  [shifted(): return lax.ppermute(x, 'context', ring)]
    ppermute x3 -> x5, starting transfers between devices: 53.9 us -> 69.1 us  [shifted(): return lax.ppermute(x, 'context', ring)]
    all_to_all x1, waiting for transfers between devices: 6.85 us -> 0.01 us  [attention(): lax.all_to_all(cross_parts, 'context', 0, 0, axis_index_groups=lines)]
    all_to_all x1, starting transfers between devices: 5.81 us -> 9.43 us  [attention(): lax.all_to_all(cross_parts, 'context', 0, 0, axis_index_groups=lines)]
    all_gather x1, waiting for transfers between devices: 0.01 us -> 2.81 us  [attention(): text = lax.all_gather(text, 'context', axis_index_groups=columns)]
    all_to_all x1, starting transfers between devices: 3.75 us -> 6.08 us  [attention(): lax.all_to_all(self_parts, 'context', 0, 0, axis_index_groups=lines)]
  transfers between devices with their start and end apart: 7 -> 9, of which waited for: 5 -> 5; matrix products, arithmetic and copies ran while one was open for 0% -> 0% of each run, Pallas kernels for 9% -> 10%
where the time goes in v6:
time: 171 us; the launch traced here: 169 us
  starting transfers between devices  91.2 us (53%)
  waiting for transfers between devices  27 us (16%)
  Pallas kernels  22 us (13%)
  between operations  14.2 us (8%)
  blocking collectives  11.4 us (7%)
  local copies, waits for them, and re-layouts  3.38 us (2%)
    ppermute x5, starting transfers between devices, shifted(): return lax.ppermute(x, 'context', ring)  69.1 us
    all_to_all x1, waiting for transfers between devices, attention(): lax.all_to_all(self_parts, 'context', 0, 0, axis_index_groups=lines)  16.8 us
    pallas_call x2, Pallas kernels, attend(): pl.pallas_call(lambda *refs: kernel(rows, *refs), grid=(RING // STEP,), i...  14.5 us
    all_to_all x1, blocking collectives, attention(): keys = lax.all_to_all(keys, 'context', 0, 0, axis_index_groups=squares)  11.4 us
    all_to_all x1, starting transfers between devices, attention(): lax.all_to_all(cross_parts, 'context', 0, 0, axis_index_groups=lines)  9.43 us
    ppermute x5, waiting for transfers between devices, shifted(): return lax.ppermute(x, 'context', ring)  7.28 us
    all_to_all x1, starting transfers between devices, attention(): queries = lax.all_to_all(queries, 'context', 0, 0, axis_index_groups=lines)  6.53 us
    all_to_all x1, starting transfers between devices, attention(): lax.all_to_all(self_parts, 'context', 0, 0, axis_index_groups=lines)  6.08 us
  transfers between devices with their start and end apart: 9, of which 5 were waited for; matrix products, arithmetic and copies ran while one was open for 0% of the time, Pallas kernels for 10%

profile of v6, /device:TPU:65, one launch (start us, length us, event | category | flops | bytes accessed | tf_op | source)
XLA Modules:
  0.0 169.1 jit_solution(15769572644178242116)
XLA Ops:
  7.2 2.5 %prepare.1 = (bf16[8,640,128]{2,1,0:T(8,128)(2,1)}, bf16[4,208,128]{2,1,0:T(8,128)(2,1)}) custom-call(s32[256]{0:T(256)} %order.3, f32[1,128]{1,0:T(1,128)} %constant.2.clone.freq, bf16[80,1024]{1,0:T(8,128)(2,1)} %sq.1, bf16[80,256]{1,0:T(8,128)(2,1)} %sk.1, bf16[80,256]{1,0:T(8,128)(2,1)} %sv.1, bf16[80,1024]{1,0:T(8,128)(2,1)} %cq.1, bf16[24,256]{1,0:T(8,128)(2,1)} %ck.1, ...), custom_call_target="tpu_custom_call" | custom-call | tf_op jit(solution)/shard_map/prepare/pallas_call | solution.py:300
  9.7 11.4 %all_to_all.20 = bf16[4,208,128]{2,1,0:T(8,128)(2,1)S(1)} all-to-all(bf16[4,208,128]{2,1,0:T(8,128)(2,1)} %get-tuple-element.7), channel_id=1, replica_groups={{0,2,16,18},{4,6,20,22},{8,10,24,26},{12,14,28,30},{32,34,48,50},{36,38..., dimensions={0} | all-to-all | bytes 425984 | tf_op jit(solution)/shard_map/all_to_all | solution.py:319
  21.1 6.5 %all-to-all-start = ((bf16[8,640,128]{2,1,0:T(8,128)(2,1)}), bf16[8,640,128]{2,1,0:T(8,128)(2,1)S(1)}, u32[]{:S(2)}, u32[]{:S(2)}) async-start(bf16[8,640,128]{2,1,0:T(8,128)(2,1)} %get-tuple-element.6), calls=%async_computation | async-start | bytes 2621440 | tf_op jit(solution)/shard_map/all_to_all | solution.py:339
  27.7 0.1 all-gather.3.cloned.1.call-start
  27.7 0.7 slice.16
  28.4 0.1 all-gather.3.cloned.1.call-update
  28.5 32.0 %collective-permute-start = (bf16[4,48,128]{2,1,0:T(8,128)(2,1)S(1)}, bf16[4,48,128]{2,1,0:T(8,128)(2,1)S(1)}, u32[]{:S(2)}, u32[]{:S(2)}) collective-permute-start(bf16[4,48,128]{2,1,0:T(8,128)(2,1)S(1)} %slice.17), channel_id=1, source_target_pairs={{0,128},{2,130},{4,132},{6,134},{8,136},{10,138},{12,140},{14,142}... | collective-permute-start | bytes 147464 | tf_op jit(solution)/shard_map/ppermute | solution.py:421
  60.4 1.5 collective-permute-done
  61.9 17.9 %collective-permute-start.3 = (bf16[8,24,128]{2,1,0:T(8,128)(2,1)S(1)}, bf16[8,24,128]{2,1,0:T(8,128)(2,1)S(1)}, u32[]{:S(2)}, u32[]{:S(2)}) collective-permute-start(bf16[8,24,128]{2,1,0:T(8,128)(2,1)S(1)} %get-tuple-element.10), channel_id=1, source_target_pairs={{0,192},{2,194},{4,196},{6,198},{8,200},{10,202},{12,204},{14,206}... | collective-permute-start | bytes 147464 | tf_op jit(solution)/shard_map/ppermute | solution.py:421
  79.8 2.0 %collective-permute-start.1 = (bf16[8,24,128]{2,1,0:T(8,128)(2,1)S(1)}, bf16[8,24,128]{2,1,0:T(8,128)(2,1)S(1)}, u32[]{:S(2)}, u32[]{:S(2)}) collective-permute-start(bf16[8,24,128]{2,1,0:T(8,128)(2,1)S(1)} %get-tuple-element.11), channel_id=1, source_target_pairs={{0,64},{2,66},{4,68},{6,70},{8,72},{10,74},{12,76},{14,78},{16,80}... | collective-permute-start | bytes 147464 | tf_op jit(solution)/shard_map/ppermute | solution.py:421
  81.8 0.0 collective-permute-done.3
  81.8 12.9 %collective-permute-start.4 = (bf16[16,24,128]{2,1,0:T(8,128)(2,1)S(1)}, bf16[16,24,128]{2,1,0:T(8,128)(2,1)S(1)}, u32[]{:S(2)}, u32[]{:S(2)}) collective-permute-start(bf16[16,24,128]{2,1,0:T(8,128)(2,1)S(1)} %pad_maximum_fusion.3), channel_id=1, source_target_pairs={{0,224},{2,226},{4,228},{6,230},{8,232},{10,234},{12,236},{14,238}... | collective-permute-start | bytes 294920 | tf_op jit(solution)/shard_map/ppermute | solution.py:421
  94.7 0.0 collective-permute-done.1
  94.8 4.3 %collective-permute-start.2 = (bf16[16,24,128]{2,1,0:T(8,128)(2,1)S(1)}, bf16[16,24,128]{2,1,0:T(8,128)(2,1)S(1)}, u32[]{:S(2)}, u32[]{:S(2)}) collective-permute-start(bf16[16,24,128]{2,1,0:T(8,128)(2,1)S(1)} %pad_maximum_fusion.2), channel_id=1, source_target_pairs={{0,32},{2,34},{4,36},{6,38},{8,40},{10,42},{12,44},{14,46},{16,48}... | collective-permute-start | bytes 294920 | tf_op jit(solution)/shard_map/ppermute | solution.py:421
  99.1 0.3 collective-permute-done.4
  99.4 5.5 %collective-permute-done.2 = bf16[16,24,128]{2,1,0:T(8,128)(2,1)S(1)} collective-permute-done((bf16[16,24,128]{2,1,0:T(8,128)(2,1)S(1)}, bf16[16,24,128]{2,1,0:T(8,128)(2,1)S(1)}, u32[]{:S(2)}, u32[]{:S(2)}) %collective-permute-start.2) | collective-permute-done | bytes 98336 | tf_op jit(solution)/shard_map/ppermute | solution.py:421
  105.0 0.0 all-to-all-done.refs_1_.refs_0_
  105.0 4.3 %shard_map.96 = bf16[8,328,128]{2,1,0:T(8,128)(2,1)} custom-call(bf16[8,640,128]{2,1,0:T(8,128)(2,1)S(1)} %all-to-all-done.refs_1_.refs_0_, bf16[32,24,128]{2,1,0:T(8,128)(2,1)S(1)} %pad_maximum_fusion.refs_1_, bf16[32,24,128]{2,1,0:T(8,128)(2,1)S(1)} %pad_maximum_fusion.1.refs_2_), custom_call_target="tpu_custom_call" | custom-call | flops 3355443200 | bytes 1703936 | tf_op jit(solution)/shard_map/pallas_call | solution.py:354
  109.3 0.0 copy-start
  109.3 9.4 %all-to-all-start.3 = ((bf16[8,328,128]{2,1,0:T(8,128)(2,1)}), bf16[8,328,128]{2,1,0:T(8,128)(2,1)S(1)}, u32[]{:S(2)}, u32[]{:S(2)}) async-start(bf16[8,328,128]{2,1,0:T(8,128)(2,1)} %shard_map.96), calls=%async_computation.3 | async-start | bytes 1343488 | tf_op jit(solution)/shard_map/all_to_all | solution.py:384
  118.8 1.5 places.1
  120.2 2.8 %all-gather.3.cloned.1.call-done.refs_2_ = bf16[32,160,128]{2,1,0:T(8,128)(2,1)} async-done(((bf16[4,160,128]{2,1,0:T(8,128)(2,1)}), bf16[32,160,128]{2,1,0:T(8,128)(2,1)}) %all-gather.3.cloned.1.call-update) | async-done | bytes 1310736 | tf_op jit(solution)/shard_map/all_gather | solution.py:321
  123.0 0.0 copy-done
  123.0 0.0 copy-start.1
  123.0 1.3 copy-done.1
  124.3 0.0 copy-start.2
  124.4 0.7 copy-done.2
  125.0 0.0 copy-start.3
  125.0 0.7 copy-done.3
  125.7 10.1 %shard_map.95 = bf16[8,328,128]{2,1,0:T(8,128)(2,1)} custom-call(s32[256]{0:T(256)S(1)} %copy-done, bf16[8,640,128]{2,1,0:T(8,128)(2,1)S(1)} %all-to-all-done.refs_1_.refs_0_, bf16[32,160,128]{2,1,0:T(8,128)(2,1)S(1)} %copy-done.1, s32[1,1280]{1,0:T(1,128)S(1)} %copy-done.2, s32[1,1280]{1,0:T(1,128)S(1)} %copy-done.3), custom_call_target="tpu_custom_call" | custom-call | flops 3355443200 | bytes 1703936 | tf_op jit(solution)/shard_map/pallas_call | solution.py:354
  135.8 0.0 all-to-all-done.3.parts
  135.8 6.1 %all-to-all-start.2 = ((bf16[8,328,128]{2,1,0:T(8,128)(2,1)}), bf16[8,328,128]{2,1,0:T(8,128)(2,1)S(1)}, u32[]{:S(2)}, u32[]{:S(2)}) async-start(bf16[8,328,128]{2,1,0:T(8,128)(2,1)} %shard_map.95), calls=%async_computation.2 | async-start | bytes 1343488 | tf_op jit(solution)/shard_map/all_to_all | solution.py:393
  141.9 1.5 cross_combine.1
  143.4 16.8 %all-to-all-done.2.parts = bf16[8,328,128]{2,1,0:T(8,128)(2,1)S(1)} async-done(((bf16[8,328,128]{2,1,0:T(8,128)(2,1)}), bf16[8,328,128]{2,1,0:T(8,128)(2,1)S(1)}, u32[]{:S(2)}, u32[]{:S(2)}) %all-to-all-start.2) | async-done | bytes 671776 | tf_op jit(solution)/shard_map/all_to_all | solution.py:393
  160.2 2.0 %self_combine.1 = bf16[80,1024]{1,0:T(8,128)(2,1)} custom-call(s32[256]{0:T(256)S(1)} %copy-done, bf16[8,328,128]{2,1,0:T(8,128)(2,1)S(1)} %all-to-all-done.2.parts), custom_call_target="tpu_custom_call" | custom-call | tf_op jit(solution)/shard_map/self_combine/pallas_call | solution.py:404
  (6 shorter events, 0.1 us)
Async XLA Ops:
  21.1 83.9 %all-to-all-start = ((bf16[8,640,128]{2,1,0:T(8,128)(2,1)}), bf16[8,640,128]{2,1,0:T(8,128)(2,1)S(1)}, u32[]{:S(2)}, u32[]{:S(2)}) async-start(bf16[8,640,128]{2,1,0:T(8,128)(2,1)} %get-tuple-element.6), calls=%async_computation | async-start | bytes 2621440 | tf_op jit(solution)/shard_map/all_to_all | solution.py:339
  27.7 95.4 %all-gather.3.cloned.1.call-start = ((), (), s32[]{:S(2)}) async-start(), calls=%async_computation.4 | async-start | bytes 1474560 | tf_op jit(solution)/shard_map/all_gather | solution.py:321
  28.5 33.4 %collective-permute-start = (bf16[4,48,128]{2,1,0:T(8,128)(2,1)S(1)}, bf16[4,48,128]{2,1,0:T(8,128)(2,1)S(1)}, u32[]{:S(2)}, u32[]{:S(2)}) collective-permute-start(bf16[4,48,128]{2,1,0:T(8,128)(2,1)S(1)} %slice.17), channel_id=1, source_target_pairs={{0,128},{2,130},{4,132},{6,134},{8,136},{10,138},{12,140},{14,142}... | collective-permute-start | bytes 147464 | tf_op jit(solution)/shard_map/ppermute | solution.py:421
  61.9 19.9 %collective-permute-start.3 = (bf16[8,24,128]{2,1,0:T(8,128)(2,1)S(1)}, bf16[8,24,128]{2,1,0:T(8,128)(2,1)S(1)}, u32[]{:S(2)}, u32[]{:S(2)}) collective-permute-start(bf16[8,24,128]{2,1,0:T(8,128)(2,1)S(1)} %get-tuple-element.10), channel_id=1, source_target_pairs={{0,192},{2,194},{4,196},{6,198},{8,200},{10,202},{12,204},{14,206}... | collective-permute-start | bytes 147464 | tf_op jit(solution)/shard_map/ppermute | solution.py:421
  79.8 14.9 %collective-permute-start.1 = (bf16[8,24,128]{2,1,0:T(8,128)(2,1)S(1)}, bf16[8,24,128]{2,1,0:T(8,128)(2,1)S(1)}, u32[]{:S(2)}, u32[]{:S(2)}) collective-permute-start(bf16[8,24,128]{2,1,0:T(8,128)(2,1)S(1)} %get-tuple-element.11), channel_id=1, source_target_pairs={{0,64},{2,66},{4,68},{6,70},{8,72},{10,74},{12,76},{14,78},{16,80}... | collective-permute-start | bytes 147464 | tf_op jit(solution)/shard_map/ppermute | solution.py:421
  81.8 17.6 %collective-permute-start.4 = (bf16[16,24,128]{2,1,0:T(8,128)(2,1)S(1)}, bf16[16,24,128]{2,1,0:T(8,128)(2,1)S(1)}, u32[]{:S(2)}, u32[]{:S(2)}) collective-permute-start(bf16[16,24,128]{2,1,0:T(8,128)(2,1)S(1)} %pad_maximum_fusion.3), channel_id=1, source_target_pairs={{0,224},{2,226},{4,228},{6,230},{8,232},{10,234},{12,236},{14,238}... | collective-permute-start | bytes 294920 | tf_op jit(solution)/shard_map/ppermute | solution.py:421
  94.8 10.2 %collective-permute-start.2 = (bf16[16,24,128]{2,1,0:T(8,128)(2,1)S(1)}, bf16[16,24,128]{2,1,0:T(8,128)(2,1)S(1)}, u32[]{:S(2)}, u32[]{:S(2)}) collective-permute-start(bf16[16,24,128]{2,1,0:T(8,128)(2,1)S(1)} %pad_maximum_fusion.2), channel_id=1, source_target_pairs={{0,32},{2,34},{4,36},{6,38},{8,40},{10,42},{12,44},{14,46},{16,48}... | collective-permute-start | bytes 294920 | tf_op jit(solution)/shard_map/ppermute | solution.py:421
  109.3 13.7 %copy-start = (s32[256]{0:T(256)S(1)}, s32[256]{0:T(256)}, u32[]{:S(2)}) copy-start(s32[256]{0:T(256)} %order.3) | copy-start | bytes 3076
  109.3 26.5 %all-to-all-start.3 = ((bf16[8,328,128]{2,1,0:T(8,128)(2,1)}), bf16[8,328,128]{2,1,0:T(8,128)(2,1)S(1)}, u32[]{:S(2)}, u32[]{:S(2)}) async-start(bf16[8,328,128]{2,1,0:T(8,128)(2,1)} %shard_map.96), calls=%async_computation.3 | async-start | bytes 1343488 | tf_op jit(solution)/shard_map/all_to_all | solution.py:384
  123.0 1.3 copy-start.1
  124.3 0.7 copy-start.2
  125.0 0.7 copy-start.3
  135.8 24.4 %all-to-all-start.2 = ((bf16[8,328,128]{2,1,0:T(8,128)(2,1)}), bf16[8,328,128]{2,1,0:T(8,128)(2,1)S(1)}, u32[]{:S(2)}, u32[]{:S(2)}) async-start(bf16[8,328,128]{2,1,0:T(8,128)(2,1)} %shard_map.95), calls=%async_computation.2 | async-start | bytes 1343488 | tf_op jit(solution)/shard_map/all_to_all | solution.py:393
Sparse Core Ops, SparseCore 0:
  31.1 91.8 all-gather.2

commit v7 on v6

--- a/solution.py
+++ b/solution.py
@@ -64,10 +64,8 @@
     return ref[:, head * HEAD_DIM : (head + 1) * HEAD_DIM].astype(F32)
 
 
-def prepare_kernel(order, freq, sq, sk, sv, cq, ck, cv, q_out, kv_out):
-    rows = sq.shape[0]
-    span = rows // 2
-    ordered, rotated = local_order(order, freq, rows)
+def key_kernel(order, freq, sk, sv, ck, cv, kv_out):
+    ordered, rotated = local_order(order, freq, sk.shape[0])
     kv_local = sk.shape[1] // HEAD_DIM
     for kv in range(kv_local):
         block = rows_of(
@@ -75,6 +73,13 @@
         ).astype(BF16)
         for m in range(kv, kv_out.shape[0], kv_local):
             kv_out[m] = block
+
+
+def query_kernel(order, freq, sq, cq, q_out):
+    rows = sq.shape[0]
+    span = rows // 2
+    _, rotated = local_order(order, freq, rows)
+    kv_local = sq.shape[1] // (HEAD_DIM * GROUP)
     for kv in range(kv_local):
         heads = range(kv * GROUP, (kv + 1) * GROUP)
         turned = [rotated(sq, head) for head in heads]
@@ -297,26 +302,22 @@
     kv_rows = 2 * (rows + image)
     size = GROUP * rows
 
-    queries, keys = pl.pallas_call(
-        prepare_kernel,
-        in_specs=[whole(pltpu.SMEM)] + [whole()] * 7,
-        out_specs=[whole(), whole()],
-        out_shape=[
-            jax.ShapeDtypeStruct((RING, 2 * size, HEAD_DIM), BF16),
-            jax.ShapeDtypeStruct((PAIR * PAIR, kv_rows, HEAD_DIM), BF16),
-        ],
-        name="prepare",
-    )(
-        span_order,
-        jnp.asarray(frequencies()),
-        self_queries,
-        self_keys,
-        self_values,
-        cross_queries,
-        cross_keys,
-        cross_values,
-    )
+    freq = jnp.asarray(frequencies())
+    keys = pl.pallas_call(
+        key_kernel,
+        in_specs=[whole(pltpu.SMEM)] + [whole()] * 5,
+        out_specs=whole(),
+        out_shape=jax.ShapeDtypeStruct((PAIR * PAIR, kv_rows, HEAD_DIM), BF16),
+        name="keys",
+    )(span_order, freq, self_keys, self_values, cross_keys, cross_values)
     keys = lax.all_to_all(keys, "context", 0, 0, axis_index_groups=squares)
+    queries = pl.pallas_call(
+        query_kernel,
+        in_specs=[whole(pltpu.SMEM)] + [whole()] * 3,
+        out_specs=whole(),
+        out_shape=jax.ShapeDtypeStruct((RING, 2 * size, HEAD_DIM), BF16),
+        name="queries",
+    )(span_order, freq, self_queries, cross_queries)
     text, picture = keys[:, : 2 * rows, :], keys[:, 2 * rows :, :]
     text = lax.all_gather(text, "context", axis_index_groups=columns)
     turns = height // PAIR

time: 171 us -> 170 us (level)
  blocking collectives: 11.4 us -> 0 us
  starting transfers between devices: 91.2 us -> 98.3 us
    all_to_all x1 -> x0, blocking collectives: 11.4 us -> none  [attention(): keys = lax.all_to_all(keys, 'context', 0, 0, axis_index_groups=squares)]
    all_to_all x0 -> x1, starting transfers between devices: none -> 6.97 us  [attention(): keys = lax.all_to_all(keys, 'context', 0, 0, axis_index_groups=squares)]
    pallas_call x1 -> x2, Pallas kernels: 2.53 us -> 4.13 us  [the longest x1 2.4 us: attention(): pl.pallas_call(query_kernel, in_specs=[whole(pltpu.SMEM)] + [whole()] * 3...]
  transfers between devices with their start and end apart: 9 -> 10, of which waited for: 5 -> 5; matrix products, arithmetic and copies ran while one was open for 0% -> 0% of each run, Pallas kernels for 10% -> 12%
where the time goes in v7:
time: 170 us; the launch traced here: 168 us
  starting transfers between devices  98.3 us (58%)
  waiting for transfers between devices  28.6 us (17%)
  Pallas kernels  23.6 us (14%)
  between operations  14.2 us (8%)
  local copies, waits for them, and re-layouts  3.38 us (2%)
    ppermute x5, starting transfers between devices, shifted(): return lax.ppermute(x, 'context', ring)  68.8 us
    all_to_all x1, waiting for transfers between devices, attention(): lax.all_to_all(self_parts, 'context', 0, 0, axis_index_groups=lines)  16.8 us
    pallas_call x2, Pallas kernels, attend(): pl.pallas_call(lambda *refs: kernel(rows, *refs), grid=(RING // STEP,), i...  14.5 us
    all_to_all x1, starting transfers between devices, attention(): lax.all_to_all(cross_parts, 'context', 0, 0, axis_index_groups=lines)  8.66 us
    all_to_all x1, starting transfers between devices, attention(): keys = lax.all_to_all(keys, 'context', 0, 0, axis_index_groups=squares)  6.97 us
    all_to_all x1, starting transfers between devices, attention(): lax.all_to_all(self_parts, 'context', 0, 0, axis_index_groups=lines)  6.88 us
    all_to_all x1, starting transfers between devices, attention(): queries = lax.all_to_all(queries, 'context', 0, 0, axis_index_groups=lines)  6.87 us
    ppermute x5, waiting for transfers between devices, shifted(): return lax.ppermute(x, 'context', ring)  6.41 us
  transfers between devices with their start and end apart: 10, of which 5 were waited for; matrix products, arithmetic and copies ran while one was open for 0% of the time, Pallas kernels for 12%

profile of v7, /device:TPU:65, one launch (start us, length us, event | category | flops | bytes accessed | tf_op | source)
XLA Modules:
  0.0 168.1 jit_solution(16646300398265287095)
XLA Ops:
  7.2 1.7 %keys.1 = bf16[4,208,128]{2,1,0:T(8,128)(2,1)} custom-call(s32[256]{0:T(256)} %order.5, f32[1,128]{1,0:T(1,128)} %constant.2.clone.freq, bf16[80,256]{1,0:T(8,128)(2,1)} %sk.1, bf16[80,256]{1,0:T(8,128)(2,1)} %sv.1, bf16[24,256]{1,0:T(8,128)(2,1)} %ck.1, bf16[24,256]{1,0:T(8,128)(2,1)} %cv.1), custom_call_target="tpu_custom_call" | custom-call | tf_op jit(solution)/shard_map/keys/pallas_call | solution.py:306
  8.9 7.0 %all-to-all-start.1 = ((bf16[4,208,128]{2,1,0:T(8,128)(2,1)}), bf16[4,208,128]{2,1,0:T(8,128)(2,1)S(1)}, u32[]{:S(2)}, u32[]{:S(2)}) async-start(bf16[4,208,128]{2,1,0:T(8,128)(2,1)} %keys.1), calls=%async_computation.1 | async-start | bytes 425984 | tf_op jit(solution)/shard_map/all_to_all | solution.py:313
  15.9 2.4 %queries.1 = bf16[8,640,128]{2,1,0:T(8,128)(2,1)} custom-call(s32[256]{0:T(256)} %order.5, f32[1,128]{1,0:T(1,128)} %constant.2.clone.freq, bf16[80,1024]{1,0:T(8,128)(2,1)} %sq.1, bf16[80,1024]{1,0:T(8,128)(2,1)} %cq.1), custom_call_target="tpu_custom_call" | custom-call | tf_op jit(solution)/shard_map/queries/pallas_call | solution.py:314
  18.3 1.7 %all-to-all-done.1 = bf16[4,208,128]{2,1,0:T(8,128)(2,1)S(1)} async-done(((bf16[4,208,128]{2,1,0:T(8,128)(2,1)}), bf16[4,208,128]{2,1,0:T(8,128)(2,1)S(1)}, u32[]{:S(2)}, u32[]{:S(2)}) %all-to-all-start.1) | async-done | bytes 213024 | tf_op jit(solution)/shard_map/all_to_all | solution.py:313
  20.0 6.9 %all-to-all-start = ((bf16[8,640,128]{2,1,0:T(8,128)(2,1)}), bf16[8,640,128]{2,1,0:T(8,128)(2,1)S(1)}, u32[]{:S(2)}, u32[]{:S(2)}) async-start(bf16[8,640,128]{2,1,0:T(8,128)(2,1)} %queries.1), calls=%async_computation | async-start | bytes 2621440 | tf_op jit(solution)/shard_map/all_to_all | solution.py:340
  26.8 0.1 all-gather.3.cloned.1.call-start
  26.9 0.7 slice.16
  27.6 0.1 all-gather.3.cloned.1.call-update
  27.7 32.0 %collective-permute-start = (bf16[4,48,128]{2,1,0:T(8,128)(2,1)S(1)}, bf16[4,48,128]{2,1,0:T(8,128)(2,1)S(1)}, u32[]{:S(2)}, u32[]{:S(2)}) collective-permute-start(bf16[4,48,128]{2,1,0:T(8,128)(2,1)S(1)} %slice.17), channel_id=1, source_target_pairs={{0,128},{2,130},{4,132},{6,134},{8,136},{10,138},{12,140},{14,142}... | collective-permute-start | bytes 147464 | tf_op jit(solution)/shard_map/ppermute | solution.py:422
  59.6 1.5 collective-permute-done
  61.1 18.9 %collective-permute-start.3 = (bf16[8,24,128]{2,1,0:T(8,128)(2,1)S(1)}, bf16[8,24,128]{2,1,0:T(8,128)(2,1)S(1)}, u32[]{:S(2)}, u32[]{:S(2)}) collective-permute-start(bf16[8,24,128]{2,1,0:T(8,128)(2,1)S(1)} %get-tuple-element.6), channel_id=1, source_target_pairs={{0,192},{2,194},{4,196},{6,198},{8,200},{10,202},{12,204},{14,206}... | collective-permute-start | bytes 147464 | tf_op jit(solution)/shard_map/ppermute | solution.py:422
  80.1 2.0 %collective-permute-start.1 = (bf16[8,24,128]{2,1,0:T(8,128)(2,1)S(1)}, bf16[8,24,128]{2,1,0:T(8,128)(2,1)S(1)}, u32[]{:S(2)}, u32[]{:S(2)}) collective-permute-start(bf16[8,24,128]{2,1,0:T(8,128)(2,1)S(1)} %get-tuple-element.7), channel_id=1, source_target_pairs={{0,64},{2,66},{4,68},{6,70},{8,72},{10,74},{12,76},{14,78},{16,80}... | collective-permute-start | bytes 147464 | tf_op jit(solution)/shard_map/ppermute | solution.py:422
  82.0 0.0 collective-permute-done.3
  82.1 10.9 %collective-permute-start.4 = (bf16[16,24,128]{2,1,0:T(8,128)(2,1)S(1)}, bf16[16,24,128]{2,1,0:T(8,128)(2,1)S(1)}, u32[]{:S(2)}, u32[]{:S(2)}) collective-permute-start(bf16[16,24,128]{2,1,0:T(8,128)(2,1)S(1)} %pad_maximum_fusion.3), channel_id=1, source_target_pairs={{0,224},{2,226},{4,228},{6,230},{8,232},{10,234},{12,236},{14,238}... | collective-permute-start | bytes 294920 | tf_op jit(solution)/shard_map/ppermute | solution.py:422
  92.9 0.0 collective-permute-done.1
  93.0 5.1 %collective-permute-start.2 = (bf16[16,24,128]{2,1,0:T(8,128)(2,1)S(1)}, bf16[16,24,128]{2,1,0:T(8,128)(2,1)S(1)}, u32[]{:S(2)}, u32[]{:S(2)}) collective-permute-start(bf16[16,24,128]{2,1,0:T(8,128)(2,1)S(1)} %pad_maximum_fusion.2), channel_id=1, source_target_pairs={{0,32},{2,34},{4,36},{6,38},{8,40},{10,42},{12,44},{14,46},{16,48}... | collective-permute-start | bytes 294920 | tf_op jit(solution)/shard_map/ppermute | solution.py:422
  98.1 0.0 collective-permute-done.4
  98.1 4.9 %collective-permute-done.2 = bf16[16,24,128]{2,1,0:T(8,128)(2,1)S(1)} collective-permute-done((bf16[16,24,128]{2,1,0:T(8,128)(2,1)S(1)}, bf16[16,24,128]{2,1,0:T(8,128)(2,1)S(1)}, u32[]{:S(2)}, u32[]{:S(2)}) %collective-permute-start.2) | collective-permute-done | bytes 98336 | tf_op jit(solution)/shard_map/ppermute | solution.py:422
  103.1 0.0 all-to-all-done.refs_1_.refs_0_
  103.1 4.3 %shard_map.96 = bf16[8,328,128]{2,1,0:T(8,128)(2,1)} custom-call(bf16[8,640,128]{2,1,0:T(8,128)(2,1)S(1)} %all-to-all-done.refs_1_.refs_0_, bf16[32,24,128]{2,1,0:T(8,128)(2,1)S(1)} %pad_maximum_fusion.refs_1_, bf16[32,24,128]{2,1,0:T(8,128)(2,1)S(1)} %pad_maximum_fusion.1.refs_2_), custom_call_target="tpu_custom_call" | custom-call | flops 3355443200 | bytes 1703936 | tf_op jit(solution)/shard_map/pallas_call | solution.py:355
  107.4 0.0 copy-start
  107.4 8.7 %all-to-all-start.3 = ((bf16[8,328,128]{2,1,0:T(8,128)(2,1)}), bf16[8,328,128]{2,1,0:T(8,128)(2,1)S(1)}, u32[]{:S(2)}, u32[]{:S(2)}) async-start(bf16[8,328,128]{2,1,0:T(8,128)(2,1)} %shard_map.96), calls=%async_computation.3 | async-start | bytes 1343488 | tf_op jit(solution)/shard_map/all_to_all | solution.py:385
  116.1 1.5 places.1
  117.6 3.7 %all-gather.3.cloned.1.call-done.refs_2_ = bf16[32,160,128]{2,1,0:T(8,128)(2,1)} async-done(((bf16[4,160,128]{2,1,0:T(8,128)(2,1)}), bf16[32,160,128]{2,1,0:T(8,128)(2,1)}) %all-gather.3.cloned.1.call-update) | async-done | bytes 1310736 | tf_op jit(solution)/shard_map/all_gather | solution.py:322
  121.2 0.0 copy-done
  121.2 0.0 copy-start.1
  121.2 1.3 copy-done.1
  122.6 0.0 copy-start.2
  122.6 0.7 copy-done.2
  123.2 0.0 copy-start.3
  123.2 0.7 copy-done.3
  123.9 10.1 %shard_map.95 = bf16[8,328,128]{2,1,0:T(8,128)(2,1)} custom-call(s32[256]{0:T(256)S(1)} %copy-done, bf16[8,640,128]{2,1,0:T(8,128)(2,1)S(1)} %all-to-all-done.refs_1_.refs_0_, bf16[32,160,128]{2,1,0:T(8,128)(2,1)S(1)} %copy-done.1, s32[1,1280]{1,0:T(1,128)S(1)} %copy-done.2, s32[1,1280]{1,0:T(1,128)S(1)} %copy-done.3), custom_call_target="tpu_custom_call" | custom-call | flops 3355443200 | bytes 1703936 | tf_op jit(solution)/shard_map/pallas_call | solution.py:355
  134.1 0.0 all-to-all-done.3.parts
  134.1 6.9 %all-to-all-start.2 = ((bf16[8,328,128]{2,1,0:T(8,128)(2,1)}), bf16[8,328,128]{2,1,0:T(8,128)(2,1)S(1)}, u32[]{:S(2)}, u32[]{:S(2)}) async-start(bf16[8,328,128]{2,1,0:T(8,128)(2,1)} %shard_map.95), calls=%async_computation.2 | async-start | bytes 1343488 | tf_op jit(solution)/shard_map/all_to_all | solution.py:394
  140.9 1.5 cross_combine.1
  142.4 16.8 %all-to-all-done.2.parts = bf16[8,328,128]{2,1,0:T(8,128)(2,1)S(1)} async-done(((bf16[8,328,128]{2,1,0:T(8,128)(2,1)}), bf16[8,328,128]{2,1,0:T(8,128)(2,1)S(1)}, u32[]{:S(2)}, u32[]{:S(2)}) %all-to-all-start.2) | async-done | bytes 671776 | tf_op jit(solution)/shard_map/all_to_all | solution.py:394
  159.2 2.0 %self_combine.1 = bf16[80,1024]{1,0:T(8,128)(2,1)} custom-call(s32[256]{0:T(256)S(1)} %copy-done, bf16[8,328,128]{2,1,0:T(8,128)(2,1)S(1)} %all-to-all-done.2.parts), custom_call_target="tpu_custom_call" | custom-call | tf_op jit(solution)/shard_map/self_combine/pallas_call | solution.py:405
  (6 shorter events, 0.1 us)
Async XLA Ops:
  8.9 11.1 %all-to-all-start.1 = ((bf16[4,208,128]{2,1,0:T(8,128)(2,1)}), bf16[4,208,128]{2,1,0:T(8,128)(2,1)S(1)}, u32[]{:S(2)}, u32[]{:S(2)}) async-start(bf16[4,208,128]{2,1,0:T(8,128)(2,1)} %keys.1), calls=%async_computation.1 | async-start | bytes 425984 | tf_op jit(solution)/shard_map/all_to_all | solution.py:313
  20.0 83.1 %all-to-all-start = ((bf16[8,640,128]{2,1,0:T(8,128)(2,1)}), bf16[8,640,128]{2,1,0:T(8,128)(2,1)S(1)}, u32[]{:S(2)}, u32[]{:S(2)}) async-start(bf16[8,640,128]{2,1,0:T(8,128)(2,1)} %queries.1), calls=%async_computation | async-start | bytes 2621440 | tf_op jit(solution)/shard_map/all_to_all | solution.py:340
  26.8 94.4 %all-gather.3.cloned.1.call-start = ((), (), s32[]{:S(2)}) async-start(), calls=%async_computation.4 | async-start | bytes 1474560 | tf_op jit(solution)/shard_map/all_gather | solution.py:322
  27.7 33.4 %collective-permute-start = (bf16[4,48,128]{2,1,0:T(8,128)(2,1)S(1)}, bf16[4,48,128]{2,1,0:T(8,128)(2,1)S(1)}, u32[]{:S(2)}, u32[]{:S(2)}) collective-permute-start(bf16[4,48,128]{2,1,0:T(8,128)(2,1)S(1)} %slice.17), channel_id=1, source_target_pairs={{0,128},{2,130},{4,132},{6,134},{8,136},{10,138},{12,140},{14,142}... | collective-permute-start | bytes 147464 | tf_op jit(solution)/shard_map/ppermute | solution.py:422
  61.1 20.9 %collective-permute-start.3 = (bf16[8,24,128]{2,1,0:T(8,128)(2,1)S(1)}, bf16[8,24,128]{2,1,0:T(8,128)(2,1)S(1)}, u32[]{:S(2)}, u32[]{:S(2)}) collective-permute-start(bf16[8,24,128]{2,1,0:T(8,128)(2,1)S(1)} %get-tuple-element.6), channel_id=1, source_target_pairs={{0,192},{2,194},{4,196},{6,198},{8,200},{10,202},{12,204},{14,206}... | collective-permute-start | bytes 147464 | tf_op jit(solution)/shard_map/ppermute | solution.py:422
  80.1 12.9 %collective-permute-start.1 = (bf16[8,24,128]{2,1,0:T(8,128)(2,1)S(1)}, bf16[8,24,128]{2,1,0:T(8,128)(2,1)S(1)}, u32[]{:S(2)}, u32[]{:S(2)}) collective-permute-start(bf16[8,24,128]{2,1,0:T(8,128)(2,1)S(1)} %get-tuple-element.7), channel_id=1, source_target_pairs={{0,64},{2,66},{4,68},{6,70},{8,72},{10,74},{12,76},{14,78},{16,80}... | collective-permute-start | bytes 147464 | tf_op jit(solution)/shard_map/ppermute | solution.py:422
  82.1 16.0 %collective-permute-start.4 = (bf16[16,24,128]{2,1,0:T(8,128)(2,1)S(1)}, bf16[16,24,128]{2,1,0:T(8,128)(2,1)S(1)}, u32[]{:S(2)}, u32[]{:S(2)}) collective-permute-start(bf16[16,24,128]{2,1,0:T(8,128)(2,1)S(1)} %pad_maximum_fusion.3), channel_id=1, source_target_pairs={{0,224},{2,226},{4,228},{6,230},{8,232},{10,234},{12,236},{14,238}... | collective-permute-start | bytes 294920 | tf_op jit(solution)/shard_map/ppermute | solution.py:422
  93.0 10.1 %collective-permute-start.2 = (bf16[16,24,128]{2,1,0:T(8,128)(2,1)S(1)}, bf16[16,24,128]{2,1,0:T(8,128)(2,1)S(1)}, u32[]{:S(2)}, u32[]{:S(2)}) collective-permute-start(bf16[16,24,128]{2,1,0:T(8,128)(2,1)S(1)} %pad_maximum_fusion.2), channel_id=1, source_target_pairs={{0,32},{2,34},{4,36},{6,38},{8,40},{10,42},{12,44},{14,46},{16,48}... | collective-permute-start | bytes 294920 | tf_op jit(solution)/shard_map/ppermute | solution.py:422
  107.4 13.8 %copy-start = (s32[256]{0:T(256)S(1)}, s32[256]{0:T(256)}, u32[]{:S(2)}) copy-start(s32[256]{0:T(256)} %order.5) | copy-start | bytes 3076
  107.4 26.6 %all-to-all-start.3 = ((bf16[8,328,128]{2,1,0:T(8,128)(2,1)}), bf16[8,328,128]{2,1,0:T(8,128)(2,1)S(1)}, u32[]{:S(2)}, u32[]{:S(2)}) async-start(bf16[8,328,128]{2,1,0:T(8,128)(2,1)} %shard_map.96), calls=%async_computation.3 | async-start | bytes 1343488 | tf_op jit(solution)/shard_map/all_to_all | solution.py:385
  121.2 1.3 copy-start.1
  122.6 0.7 copy-start.2
  123.2 0.7 copy-start.3
  134.1 25.2 %all-to-all-start.2 = ((bf16[8,328,128]{2,1,0:T(8,128)(2,1)}), bf16[8,328,128]{2,1,0:T(8,128)(2,1)S(1)}, u32[]{:S(2)}, u32[]{:S(2)}) async-start(bf16[8,328,128]{2,1,0:T(8,128)(2,1)} %shard_map.95), calls=%async_computation.2 | async-start | bytes 1343488 | tf_op jit(solution)/shard_map/all_to_all | solution.py:394
Sparse Core Ops, SparseCore 0:
  30.3 90.8 all-gather.2
